TPU v7x, 64 devices: a 2x2x8 block of a 4x4x8 slice. The times are simulated.
64 devices in a mesh: dp: 4 (over x, y), ep: 16 (over z, core).
Axes of the slice: x: 2, y: 2, z: 8, core: 2. Of those that a mesh axis runs over, the one named last changes fastest.
The devices are a block of a 4x4x8 slice.
Arguments:
- x_in: bfloat16 [192, 512, 768], P(('dp', 'ep')), parts along dimension 0
- pad_mask: int32 [192, 512], P(('dp', 'ep')), parts along dimension 0
- rel_bias: float32 [12, 512, 512], replicated
- expert_idx: int32 [2, 192, 512], P(None, ('dp', 'ep')), parts along dimension 1
- norm_scale: float32 [2, 2, 768], replicated
- w_query: bfloat16 [2, 768, 768], replicated
- w_key: bfloat16 [2, 768, 768], replicated
- w_value: bfloat16 [2, 768, 768], replicated
- w_attn_out: bfloat16 [2, 768, 768], replicated
- w_router: float32 [2, 768, 64], replicated
- w_in: bfloat16 [2, 64, 768, 3072], P(None, 'ep')
- w_out: bfloat16 [2, 64, 3072, 768], P(None, 'ep')
Outputs:
- output: bfloat16 [192, 512, 768], P(('dp', 'ep')), parts along dimension 0
There are 4 independent parts. A program takes and returns all parts, laid end to end along the dimension named above; an argument that names none is the same for every part.
All inputs are finite; a program needn't handle non-finite values.
Results may differ from a plain program's by a relative error of at most 0.0196086.
Values are sent between devices in bfloat16 or wider.
A program may use at most 768 MiB of HBM per device.

v0:
```python
import jax
import jax.numpy as jnp
from jax import lax
from jax.sharding import PartitionSpec as P, NamedSharding

NORM_EPS = 1e-6
NEG_BIG = -1e9
CAP_FACTOR = 2


def rms_norm(hidden, gain):
    hid32 = hidden.astype(jnp.float32)
    return hid32 * lax.rsqrt(jnp.mean(hid32 * hid32, axis=-1, keepdims=True) + NORM_EPS) * gain


def attention(hidden, pad_mask, rel_bias, gain, query_w, key_w, value_w, out_w):
    num_seqs, seq_len, model_dim = hidden.shape
    num_heads = rel_bias.shape[0]
    head_dim = query_w.shape[1] // num_heads
    normed = rms_norm(hidden, gain).astype(jnp.bfloat16)

    def project(weight):
        out_rows = jnp.einsum('std,de->ste', normed, weight, preferred_element_type=jnp.float32)
        return out_rows.astype(jnp.bfloat16).reshape(num_seqs, seq_len, num_heads, head_dim)

    query_rows = project(query_w)
    key_rows = project(key_w)
    value_rows = project(value_w)
    scores = jnp.einsum('sqhd,skhd->shqk', query_rows, key_rows, preferred_element_type=jnp.float32)
    scores = scores + rel_bias[None] + jnp.where(pad_mask > 0, 0.0, NEG_BIG)[:, None, None, :]
    attn_probs = jax.nn.softmax(scores, axis=-1).astype(jnp.bfloat16)
    context = jnp.einsum('shqk,skhd->sqhd', attn_probs, value_rows, preferred_element_type=jnp.float32)
    context = context.astype(jnp.bfloat16).reshape(num_seqs, seq_len, num_heads * head_dim)
    attn_out = jnp.einsum('ste,ed->std', context, out_w, preferred_element_type=jnp.float32)
    return (hidden.astype(jnp.float32) + attn_out).astype(jnp.bfloat16)


def token_slots(expert_ids, num_experts):
    tok_count = expert_ids.shape[0]
    sort_order = jnp.argsort(expert_ids, stable=True)
    counts = jnp.zeros((num_experts,), jnp.int32).at[expert_ids].add(1)
    starts = jnp.cumsum(counts) - counts
    rank_sorted = jnp.arange(tok_count, dtype=jnp.int32) - starts[expert_ids[sort_order]]
    return jnp.zeros((tok_count,), jnp.int32).at[sort_order].set(rank_sorted)


def dispatch(flat_hidden, expert_ids, gain, route_w, capacity):
    tok_count, model_dim = flat_hidden.shape
    num_experts = route_w.shape[1]
    normed32 = rms_norm(flat_hidden, gain)
    logits = jnp.dot(normed32, route_w, precision=lax.Precision.HIGHEST, preferred_element_type=jnp.float32)
    gate_val = jnp.take_along_axis(jax.nn.softmax(logits, axis=-1), expert_ids[:, None], axis=1)[:, 0]
    token_slot = token_slots(expert_ids, num_experts)
    flat_slot = jnp.where(token_slot < capacity, expert_ids * capacity + token_slot, num_experts * capacity)
    slot_token = jnp.full((num_experts * capacity,), tok_count, jnp.int32).at[flat_slot].set(jnp.arange(tok_count, dtype=jnp.int32), mode='drop')
    packed = jnp.take(normed32.astype(jnp.bfloat16), slot_token, axis=0, mode='fill', fill_value=0)
    return packed.reshape(num_experts, capacity, model_dim), gate_val, flat_slot


def expert_ffn(rows_in, up_w, down_w):
    inner_act = jnp.einsum('ecd,edf->ecf', rows_in, up_w, preferred_element_type=jnp.float32)
    inner_act = jnp.maximum(inner_act, 0.0).astype(jnp.bfloat16)
    return jnp.einsum('ecf,efd->ecd', inner_act, down_w, preferred_element_type=jnp.float32).astype(jnp.bfloat16)


def combine(flat_hidden, expert_rows, gate_val, flat_slot):
    returned = jnp.take(expert_rows, flat_slot, axis=0, mode='fill', fill_value=0)
    return (flat_hidden.astype(jnp.float32) + gate_val[:, None] * returned.astype(jnp.float32)).astype(jnp.bfloat16)


def solution(mesh):
    token_spec = P(('dp', 'ep'))

    def per_device(x_in, pad_mask, rel_bias, expert_idx, norm_scale, w_query, w_key, w_value, w_attn_out, w_router, w_in, w_out):
        num_seqs, seq_len, model_dim = x_in.shape
        tok_count = num_seqs * seq_len
        num_experts = w_router.shape[2]
        capacity = (CAP_FACTOR * tok_count + num_experts - 1) // num_experts
        hidden = x_in
        for layer_id in range(w_router.shape[0]):
            hidden = attention(hidden, pad_mask, rel_bias, norm_scale[layer_id, 0], w_query[layer_id], w_key[layer_id], w_value[layer_id], w_attn_out[layer_id])
            flat_hidden = hidden.reshape(tok_count, model_dim)
            packed, gate_val, flat_slot = dispatch(flat_hidden, expert_idx[layer_id].reshape(tok_count), norm_scale[layer_id, 1], w_router[layer_id], capacity)
            received = lax.all_to_all(packed, 'ep', 0, 1, tiled=True)
            expert_rows = expert_ffn(received, w_in[layer_id], w_out[layer_id])
            returned = lax.all_to_all(expert_rows, 'ep', 1, 0, tiled=True)
            hidden = combine(flat_hidden, returned.reshape(num_experts * capacity, model_dim), gate_val, flat_slot).reshape(num_seqs, seq_len, model_dim)
        return hidden

    return jax.shard_map(per_device, mesh=mesh, in_specs=(token_spec, token_spec, P(), P(None, ('dp', 'ep')), P(), P(), P(), P(), P(), P(), P(None, 'ep'), P(None, 'ep')), out_specs=token_spec, check_vma=False)
```

profile of v0, /device:TPU:21, one launch (start us, length us, event | category | flops | bytes accessed | tf_op | source)
XLA Modules:
  0.0 884.2 jit_solution(14199135898197657608)
XLA Ops:
  3.2 11.1 %scatter_custom_fusion = s32[64]{0:T(128)S(1)} fusion(s32[1536]{0:T(1024)S(1)} %get-tuple-element.149, s32[1536]{0:T(1024)S(1)} %broadcast.496, s32[]{:T(128)} %constant.38.clone.1), kind=kCustom, calls=%fused_computation.306 | custom fusion | flops 1536 | bytes 260 | tf_op jit(solution)/shard_map/scatter-add | solution.py:41
  22.7 8.4 gather_fusion
  36.7 36.0 %select_subtract_fusion.1 = s32[1536]{0:T(1024)S(1)} fusion(pred[1536]{0:T(1024)(128)(4,1)S(1)} %get-tuple-element.131, pred[1536]{0:T(1024)(128)(4,1)S(1)} %get-tuple-element.130, pred[1536]{0:T(1024)(128)(4,1)S(1)} %get-tuple-element.129, pred[1536]{0:T(1024)(128)(4,1)S(1)} %get-tuple-element.128, pred[1536]{0:T(1024)(128)(4,1)S(1)} %get-tuple-element.127, ...), kind=kLoop, calls=%fused_computation.268 | loop fusion | flops 89088 | bytes 100068 | tf_op jit(solution)/shard_map/sub | solution.py:43
  114.5 12.6 %copy.63 = f32[12,512,512]{1,2,0:T(8,128)} copy(f32[12,512,512]{2,1,0:T(8,128)} %param.20) | data formatting | bytes 25165824 | tf_op args[2]
  127.1 22.7 %fusion.123 = (f32[3,12,512]{2,1,0:T(8,128)S(1)}, f32[3,12,512,512]{2,3,1,0:T(8,128)}) fusion(f32[3,512]{1,0:T(4,128)S(1)} %compare_select_fusion.22, f32[12,512,512]{1,2,0:T(8,128)} %copy.63, bf16[3,512,12,64]{1,3,2,0:T(8,128)(2,1)S(1)} %bitcast.283, bf16[3,512,12,64]{1,3,2,0:T(8,128)(2,1)} %bitcast.284), kind=kOutput, calls=%fused_computation.324 | convolution fusion | flops 1245708800 | bytes 55130112 | tf_op jit(solution)/shard_map/sub | solution.py:31
  149.8 16.0 %fusion.50 = bf16[3,12,64,512]{3,2,1,0:T(8,128)(2,1)} fusion(bf16[3,512,12,64]{1,3,2,0:T(8,128)(2,1)} %bitcast.297, f32[3,12,512,512]{2,3,1,0:T(8,128)} %get-tuple-element.279, f32[3,12,512]{2,1,0:T(8,128)S(1)} %get-tuple-element.278), kind=kOutput, calls=%fused_computation.82 | convolution fusion | flops 1228013568 | bytes 42541056 | tf_op jit(solution)/shard_map/shqk,skhd->sqhd/dot_general | solution.py:32
  173.8 13.5 %gather_fusion.3 = bf16[3072,768]{1,0:T(8,128)(2,1)} fusion(bf16[1536,768]{1,0:T(8,128)(2,1)S(1)} %fusion.40, s32[3072]{0:T(1024)S(1)} %fusion.82), kind=kCustom, calls=%fused_computation.1.clone | custom fusion | bytes 9449472 | tf_op jit(solution)/shard_map/jit(_take)/gather | solution.py:56
  190.6 117.5 %all_to_all.66 = bf16[64,48,768]{2,1,0:T(8,128)(2,1)S(1)} all-to-all(bf16[64,48,768]{2,1,0:T(8,128)(2,1)S(1)} %bitcast.289), channel_id=1, replica_groups=mesh['dp'=4,'ep'=16] {'ep'}, dimensions={0} | all-to-all | bytes 9437184 | tf_op jit(solution)/shard_map/all_to_all | solution.py:84
  310.7 22.1 %fusion.10 = bf16[4,768,3072]{2,1,0:T(8,128)(2,1)} fusion(bf16[4,768,768]{2,1,0:T(8,128)(2,1)} %bitcast.294, bf16[2,4,768,3072]{3,2,1,0:T(8,128)(2,1)} %param.28), kind=kOutput, calls=%fused_computation.32 | convolution fusion | flops 14495514624 | bytes 42467328 | tf_op jit(solution)/shard_map/ecd,edf->ecf/dot_general | solution.py:61
  332.7 24.8 %fusion.45 = bf16[4,768,768]{2,1,0:T(8,128)(2,1)} fusion(bf16[2,4,3072,768]{3,2,1,0:T(8,128)(2,1)} %param.29, bf16[4,768,3072]{2,1,0:T(8,128)(2,1)} %fusion.10), kind=kOutput, calls=%fused_computation.79 | convolution fusion | flops 14526185472 | bytes 42467328 | tf_op jit(solution)/shard_map/ecf,efd->ecd/dot_general | solution.py:63
  375.7 8.4 gather_fusion.1
  384.1 11.4 %scatter_custom_fusion.3 = s32[64]{0:T(128)S(1)} fusion(s32[1536]{0:T(1024)} %get-tuple-element.290, s32[1536]{0:T(1024)} %copy-done.26, s32[]{:T(128)} %constant.38.clone.1), kind=kCustom, calls=%fused_computation.304 | custom fusion | flops 1536 | bytes 768 | tf_op jit(solution)/shard_map/scatter-add | solution.py:41
  404.3 36.0 %select_subtract_fusion = s32[1536]{0:T(1024)S(1)} fusion(pred[1536]{0:T(1024)(128)(4,1)S(1)} %get-tuple-element.74, pred[1536]{0:T(1024)(128)(4,1)S(1)} %get-tuple-element.73, pred[1536]{0:T(1024)(128)(4,1)S(1)} %get-tuple-element.72, pred[1536]{0:T(1024)(128)(4,1)S(1)} %get-tuple-element.71, pred[1536]{0:T(1024)(128)(4,1)S(1)} %get-tuple-element.70, ...), kind=kLoop, calls=%fused_computation.267 | loop fusion | flops 89088 | bytes 100068 | tf_op jit(solution)/shard_map/sub | solution.py:43
  459.5 12.7 %gather_fusion.2 = f32[1536]{0:T(1024)S(1)} fusion(f32[1536,64]{0,1:T(8,128)S(1)} %fusion.70, s32[1536]{0:T(1024)S(1)} %fusion.96), kind=kCustom, calls=%fused_computation.clone | custom fusion | bytes 24576 | tf_op jit(solution)/shard_map/jit(take_along_axis)/gather | solution.py:52
  480.3 9.6 %gather_fusion.4 = bf16[1536,768]{1,0:T(8,128)(2,1)} fusion(bf16[3072,768]{1,0:T(8,128)(2,1)} %bitcast.281, s32[2048]{0:T(1024)S(1)} %pad_clamp_fusion.2), kind=kCustom, calls=%fused_computation.2.clone | custom fusion | bytes 4724736 | tf_op jit(solution)/shard_map/jit(_take)/gather | solution.py:67
  518.6 22.9 %fusion.125 = (f32[3,12,512]{2,1,0:T(8,128)S(1)}, f32[3,12,512,512]{2,3,1,0:T(8,128)}) fusion(f32[3,512]{1,0:T(4,128)S(1)} %copy-done.6, f32[12,512,512]{1,2,0:T(8,128)} %copy.63, bf16[3,512,12,64]{1,3,2,0:T(8,128)(2,1)} %bitcast.286, bf16[3,512,12,64]{1,3,2,0:T(8,128)(2,1)S(1)} %bitcast.285), kind=kOutput, calls=%fused_computation.326 | convolution fusion | flops 1245708800 | bytes 55130112 | tf_op jit(solution)/shard_map/sub | solution.py:31
  541.5 15.8 %fusion.49 = bf16[3,12,64,512]{3,2,1,0:T(8,128)(2,1)} fusion(bf16[3,512,12,64]{1,3,2,0:T(8,128)(2,1)} %bitcast.296, f32[3,12,512,512]{2,3,1,0:T(8,128)} %get-tuple-element.285, f32[3,12,512]{2,1,0:T(8,128)S(1)} %get-tuple-element.284), kind=kOutput, calls=%fused_computation.81 | convolution fusion | flops 1228013568 | bytes 42541056 | tf_op jit(solution)/shard_map/shqk,skhd->sqhd/dot_general | solution.py:32
  566.3 13.5 %gather_fusion.6 = bf16[3072,768]{1,0:T(8,128)(2,1)} fusion(bf16[1536,768]{1,0:T(8,128)(2,1)S(1)} %fusion.35, s32[3072]{0:T(1024)S(1)} %fusion.83), kind=kCustom, calls=%fused_computation.4.clone | custom fusion | bytes 9449472 | tf_op jit(solution)/shard_map/jit(_take)/gather | solution.py:56
  583.1 115.3 %all_to_all.67 = bf16[64,48,768]{2,1,0:T(8,128)(2,1)S(1)} all-to-all(bf16[64,48,768]{2,1,0:T(8,128)(2,1)S(1)} %bitcast.290), channel_id=1, replica_groups=mesh['dp'=4,'ep'=16] {'ep'}, dimensions={0} | all-to-all | bytes 9437184 | tf_op jit(solution)/shard_map/all_to_all | solution.py:84
  701.0 22.1 %fusion.7 = bf16[4,768,3072]{2,1,0:T(8,128)(2,1)} fusion(bf16[4,768,768]{2,1,0:T(8,128)(2,1)} %bitcast.295, bf16[2,4,768,3072]{3,2,1,0:T(8,128)(2,1)} %param.28), kind=kOutput, calls=%fused_computation.29 | convolution fusion | flops 14495514624 | bytes 42467328 | tf_op jit(solution)/shard_map/ecd,edf->ecf/dot_general | solution.py:61
  723.1 24.6 %fusion.42 = bf16[4,768,768]{2,1,0:T(8,128)(2,1)} fusion(bf16[2,4,3072,768]{3,2,1,0:T(8,128)(2,1)} %param.29, bf16[4,768,3072]{2,1,0:T(8,128)(2,1)} %fusion.7), kind=kOutput, calls=%fused_computation.78 | convolution fusion | flops 14526185472 | bytes 42467328 | tf_op jit(solution)/shard_map/ecf,efd->ecd/dot_general | solution.py:63
  766.5 12.7 %gather_fusion.5 = f32[1536]{0:T(1024)S(1)} fusion(f32[1536,64]{0,1:T(8,128)S(1)} %fusion.72, s32[1536]{0:T(1024)S(1)} %fusion.97), kind=kCustom, calls=%fused_computation.3.clone | custom fusion | bytes 24576 | tf_op jit(solution)/shard_map/jit(take_along_axis)/gather | solution.py:52
  779.3 85.6 %all-to-all-done.3 = bf16[4,768,768]{2,0,1:T(4,128)(2,1)} async-done(((bf16[4,768,768]{2,0,1:T(4,128)(2,1)}), bf16[4,768,768]{2,0,1:T(4,128)(2,1)}, u32[]{:S(2)}, u32[]{:S(2)}) %all-to-all-start.3) | async-done | bytes 4718624 | tf_op jit(solution)/shard_map/all_to_all | solution.py:86
  870.4 9.6 %gather_fusion.7 = bf16[1536,768]{1,0:T(8,128)(2,1)} fusion(bf16[3072,768]{1,0:T(8,128)(2,1)} %bitcast.282, s32[2048]{0:T(1024)S(1)} %pad_clamp_fusion), kind=kCustom, calls=%fused_computation.5.clone | custom fusion | bytes 4724736 | tf_op jit(solution)/shard_map/jit(_take)/gather | solution.py:67
  (164 shorter events, 198.1 us)
Async XLA Ops:
  3.2 11.1 %copy-start.26 = (s32[1536]{0:T(1024)}, s32[1536]{0:T(1024)S(1)}, u32[]{:S(2)}) copy-start(s32[1536]{0:T(1024)S(1)} %broadcast.496) | copy-start | bytes 18436
  14.5 71.3 %copy-start.25 = (s32[3,512]{1,0:T(4,128)S(1)}, s32[3,512]{1,0:T(4,128)}, u32[]{:S(2)}) copy-start(s32[3,512]{1,0:T(4,128)} %param.19) | copy-start | bytes 18436
  14.5 71.3 %copy-start.3 = (bf16[3,512,768]{2,1,0:T(8,128)(2,1)S(1)}, bf16[3,512,768]{2,1,0:T(8,128)(2,1)}, u32[]{:S(2)}) copy-start(bf16[3,512,768]{2,1,0:T(8,128)(2,1)} %param.18) | copy-start | bytes 7077892
  22.6 63.7 %copy-start.23 = (f32[2,2,768]{2,1,0:T(2,128)S(1)}, f32[2,2,768]{2,1,0:T(2,128)}, u32[]{:S(2)}) copy-start(f32[2,2,768]{2,1,0:T(2,128)} %param.22) | copy-start | bytes 36868
  79.5 6.2 copy-start.16
  85.8 41.3 %copy-start.5 = (f32[3,512]{1,0:T(4,128)}, f32[3,512]{1,0:T(4,128)S(1)}, u32[]{:S(2)}) copy-start(f32[3,512]{1,0:T(4,128)S(1)} %compare_select_fusion.22) | copy-start | bytes 18436
  149.8 16.0 %copy-start.4 = (bf16[3,512,768]{2,1,0:T(8,128)(2,1)S(1)}, bf16[3,512,768]{2,1,0:T(8,128)(2,1)}, u32[]{:S(2)}) copy-start(bf16[3,512,768]{2,1,0:T(8,128)(2,1)} %param.18) | copy-start | bytes 7077892
  365.7 109.1 %all-to-all-start.1 = ((bf16[4,768,768]{2,0,1:T(4,128)(2,1)}), bf16[4,768,768]{2,0,1:T(4,128)(2,1)}, u32[]{:S(2)}, u32[]{:S(2)}) async-start(bf16[4,768,768]{2,0,1:T(4,128)(2,1)} %copy.68), calls=%async_computation.1 | async-start | bytes 9437184 | tf_op jit(solution)/shard_map/all_to_all | solution.py:86
  370.6 82.8 %copy-start.20 = (s32[1536,1,1]{0,2,1:T(1,128)S(1)}, s32[1536,1,1]{0,2,1:T(1,128)}, u32[]{:S(2)}) copy-start(s32[1536,1,1]{0,2,1:T(1,128)} %get-tuple-element.148) | copy-start | bytes 18436
  370.6 82.8 %copy-start.21 = (s32[1536,1,1]{0,2,1:T(1,128)S(1)}, s32[1536,1,1]{0,2,1:T(1,128)}, u32[]{:S(2)}) copy-start(s32[1536,1,1]{0,2,1:T(1,128)} %get-tuple-element.291) | copy-start | bytes 18436
  375.6 78.4 %copy-start.1 = (bf16[3,512,768]{2,1,0:T(8,128)(2,1)S(1)}, bf16[3,512,768]{2,1,0:T(8,128)(2,1)}, u32[]{:S(2)}) copy-start(bf16[3,512,768]{2,1,0:T(8,128)(2,1)} %get-tuple-element.281) | copy-start | bytes 7077892
  384.1 70.6 %copy-start.7 = (f32[2,768,64]{1,2,0:T(8,128)S(1)}, f32[2,768,64]{1,2,0:T(8,128)}, u32[]{:S(2)}) copy-start(f32[2,768,64]{1,2,0:T(8,128)} %param.27) | copy-start | bytes 1179652
  447.0 12.3 %copy-start.18 = (s32[1536]{0:T(1024)}, s32[1536]{0:T(1024)S(1)}, u32[]{:S(2)}) copy-start(s32[1536]{0:T(1024)S(1)} %get-tuple-element.133) | copy-start | bytes 18436
  459.5 12.8 %copy-start.17 = (s32[1536]{0:T(1024)S(1)}, s32[1536]{0:T(1024)}, u32[]{:S(2)}) copy-start(s32[1536]{0:T(1024)} %copy-done.16) | copy-start | bytes 18436
  459.5 12.8 %copy-start.12 = (s32[1,3,512]{2,0,1:T(1,128)S(1)}, s32[1,3,512]{2,0,1:T(1,128)}, u32[]{:S(2)}) copy-start(s32[1,3,512]{2,0,1:T(1,128)} %copy-done.11) | copy-start | bytes 18436
  480.3 9.6 %copy-start.27 = (pred[1536]{0:T(1024)(128)(4,1)S(1)}, pred[1536]{0:T(1024)(128)(4,1)}, u32[]{:S(2)}) copy-start(pred[1536]{0:T(1024)(128)(4,1)} %get-tuple-element.138) | copy-start | bytes 4612
  493.4 6.8 copy-start.2
  510.0 8.6 copy-start.6
  541.5 15.8 %copy-start.31 = (bf16[2,768,768]{2,1,0:T(8,128)(2,1)S(1)}, bf16[2,768,768]{2,1,0:T(8,128)(2,1)}, u32[]{:S(2)}) copy-start(bf16[2,768,768]{2,1,0:T(8,128)(2,1)} %param.26) | copy-start | bytes 7077892
  557.3 6.7 copy-start.14
  755.9 4.9 copy-start
  755.9 109.1 %all-to-all-start.3 = ((bf16[4,768,768]{2,0,1:T(4,128)(2,1)}), bf16[4,768,768]{2,0,1:T(4,128)(2,1)}, u32[]{:S(2)}, u32[]{:S(2)}) async-start(bf16[4,768,768]{2,0,1:T(4,128)(2,1)} %copy.77), calls=%async_computation.3 | async-start | bytes 9437184 | tf_op jit(solution)/shard_map/all_to_all | solution.py:86
  766.5 12.7 %copy-start.10 = (s32[1,3,512]{2,0,1:T(1,128)S(1)}, s32[1,3,512]{2,0,1:T(1,128)}, u32[]{:S(2)}) copy-start(s32[1,3,512]{2,0,1:T(1,128)} %copy-done.9) | copy-start | bytes 18436
  870.4 9.6 %copy-start.24 = (pred[1536]{0:T(1024)(128)(4,1)S(1)}, pred[1536]{0:T(1024)(128)(4,1)}, u32[]{:S(2)}) copy-start(pred[1536]{0:T(1024)(128)(4,1)} %get-tuple-element.132) | copy-start | bytes 4612
  (10 other events, 31.7 us)
where the time goes:
time: 894 us; the launch traced here: 884 us
  blocking collectives  233 us (26%)
  matrix products  219 us (24%)
  local copies, waits for them, and re-layouts  193 us (22%)
  other arithmetic  140 us (16%)
  waiting for transfers between devices  88.1 us (10%)
  starting transfers between devices  9.6 us (1%)
    all_to_all x2, blocking collectives, per_device(): received = lax.all_to_all(packed, 'ep', 0, 1, tiled=True)  233 us
    all_to_all x2, waiting for transfers between devices, per_device(): returned = lax.all_to_all(expert_rows, 'ep', 1, 0, tiled=True)  88.1 us
    sub x2, other arithmetic, token_slots(): jnp.arange(tok_count, dtype=jnp.int32) - starts[expert_ids[sort_order]]  71.9 us
    dot_general x2, matrix products, expert_ffn(): jnp.einsum('ecf,efd->ecd', inner_act, down_w, preferred_element_type=jnp....  49.5 us
    sub x2, matrix products, attention(): attn_probs = jax.nn.softmax(scores, axis=-1).astype(jnp.bfloat16)  45.7 us
    dot_general x2, matrix products, expert_ffn(): jnp.einsum('ecd,edf->ecf', rows_in, up_w, preferred_element_type=jnp.floa...  44.2 us
    dot_general x2, matrix products, attention(): jnp.einsum('shqk,skhd->sqhd', attn_probs, value_rows, preferred_element_t...  31.8 us
    gather x2, local copies, waits for them, and re-layouts, dispatch(): jnp.take(normed32.astype(jnp.bfloat16), slot_token, axis=0, mode='fill',...  27.1 us
  transfers between devices with their start and end apart: 2, of which 2 were waited for; matrix products, arithmetic and copies ran while one was open for 14% of the time, Pallas kernels for 0%

commit v1 on v0

v1 whole, which is shorter than its diff:
```python
import functools

import jax
import jax.numpy as jnp
from jax import lax
from jax.experimental import pallas as pl
from jax.experimental.pallas import tpu as pltpu
from jax.sharding import PartitionSpec as P

NORM_EPS = 1e-6
NEG_BIG = -1e9
CAP_FACTOR = 2
LANES = 128
F32 = jnp.float32
BF16 = jnp.bfloat16


def rms(hid32, gain):
    return hid32 * lax.rsqrt(jnp.mean(hid32 * hid32, axis=-1, keepdims=True) + NORM_EPS) * gain


def slots_kernel(capacity, drop, e_ref, base_ref, pos_ref):
    layers, blocks, _ = e_ref.shape
    num_experts = base_ref.shape[1]
    row = lax.broadcasted_iota(jnp.int32, (LANES, LANES), 0)
    col = lax.broadcasted_iota(jnp.int32, (LANES, LANES), 1)
    upper = (row <= col).astype(F32).astype(BF16)
    experts = lax.broadcasted_iota(jnp.int32, (num_experts, LANES), 0)
    for layer in range(layers):
        carry = jnp.zeros((num_experts, 1), F32)
        for blk in range(blocks):
            hit = experts == e_ref[layer, blk:blk + 1, :]
            hot = hit.astype(F32)
            cum = jnp.dot(hot.astype(BF16), upper, preferred_element_type=F32) + (carry - 1.0)
            slot = jnp.sum(hot * cum, axis=0, keepdims=True)
            base = jnp.sum(hot * base_ref[0], axis=0, keepdims=True)
            carry = carry + jnp.sum(hot, axis=1, keepdims=True)
            pos_ref[layer, blk:blk + 1, :] = jnp.where(slot < capacity, base + slot, float(drop)).astype(jnp.int32)


def attn_kernel(head_dim, x_ref, mask_ref, bias_ref, g0_ref, g1_ref, wq_ref, wk_ref, wv_ref, wo_ref, wr_ref, e_ref,
                h1_ref, b_ref, gate_ref, q_s, k_s, v_s, ctx_s):
    pair = pl.program_id(0)
    seq = pl.program_id(1)
    pairs = pl.num_programs(0)
    n_pairs, width = q_s.shape[0], q_s.shape[3]

    @pl.when(pair == 0)
    def _():
        a = rms(x_ref[seq].astype(F32), g0_ref[...]).astype(BF16)
        for w_ref, dst in ((wq_ref, q_s), (wk_ref, k_s), (wv_ref, v_s)):
            rows = jnp.dot(a, w_ref[...], preferred_element_type=F32).astype(BF16)
            for j in range(n_pairs):
                dst[j, seq] = rows[:, j * width:(j + 1) * width]

    q2, k2, v2 = q_s[pair, seq], k_s[pair, seq], v_s[pair, seq]
    lane = lax.broadcasted_iota(jnp.int32, q2.shape, 1)
    mask_row = jnp.where(mask_ref[seq] > 0, 0.0, NEG_BIG)
    parts = []
    for half in range(width // head_dim):
        mine = (lane >= half * head_dim) & (lane < (half + 1) * head_dim)
        qh = jnp.where(mine, q2, jnp.zeros_like(q2))
        s = lax.dot_general(qh, k2, (((1,), (1,)), ((), ())), preferred_element_type=F32)
        s = s + bias_ref[half] + mask_row
        p = jnp.exp(s - jnp.max(s, axis=-1, keepdims=True))
        p = (p * (1.0 / jnp.sum(p, axis=-1, keepdims=True))).astype(BF16)
        o = jnp.dot(p, v2, preferred_element_type=F32)
        parts.append(jnp.where(mine, o, 0.0))
    ctx_s[seq, :, pl.ds(pl.multiple_of(pair * width, width), width)] = sum(parts).astype(BF16)

    @pl.when(pair == pairs - 1)
    def _():
        o = jnp.dot(ctx_s[seq], wo_ref[...], preferred_element_type=F32)
        h1 = (x_ref[seq].astype(F32) + o).astype(BF16)
        h1_ref[seq] = h1
        r = rms(h1.astype(F32), g1_ref[...])
        b_ref[seq] = r.astype(BF16)
        logits = jnp.dot(r, wr_ref[...], precision=lax.Precision.HIGHEST, preferred_element_type=F32)
        ex = jnp.exp(logits - jnp.max(logits, axis=-1, keepdims=True))
        chosen = lax.broadcasted_iota(jnp.int32, logits.shape, 1) == e_ref[seq]
        gate_ref[seq] = jnp.sum(jnp.where(chosen, ex, 0.0), axis=-1, keepdims=True) / jnp.sum(ex, axis=-1, keepdims=True)


def attention(layer, x, mask, rel_bias, gains, wq, wk, wv, wo, wr, e_col):
    num_seqs, seq_len, model_dim = x.shape
    num_heads = rel_bias.shape[0]
    inner = wq.shape[2]
    head_dim = inner // num_heads
    per = LANES // head_dim
    pairs = num_heads // per
    num_experts = wr.shape[2]
    full = lambda *shape: pl.BlockSpec(shape, lambda p, s: (0,) * len(shape))
    of_layer = lambda *shape: pl.BlockSpec((None,) + shape, lambda p, s: (layer,) + (0,) * len(shape))
    gain = lambda which: pl.BlockSpec((None, 1, model_dim), lambda p, s: (2 * layer + which, 0, 0))
    flops = 2 * num_seqs * seq_len * (4 * model_dim * inner + 2 * seq_len * inner)
    return pl.pallas_call(
        functools.partial(attn_kernel, head_dim),
        grid=(pairs, num_seqs),
        in_specs=[full(num_seqs, seq_len, model_dim), full(num_seqs, 1, seq_len),
                  pl.BlockSpec((per, seq_len, seq_len), lambda p, s: (p, 0, 0)), gain(0), gain(1),
                  of_layer(model_dim, inner), of_layer(model_dim, inner), of_layer(model_dim, inner),
                  of_layer(inner, model_dim), of_layer(model_dim, num_experts), of_layer(num_seqs, seq_len, 1)],
        out_specs=[full(num_seqs, seq_len, model_dim), full(num_seqs, seq_len, model_dim), full(num_seqs, seq_len, 1)],
        out_shape=[jax.ShapeDtypeStruct(x.shape, BF16), jax.ShapeDtypeStruct(x.shape, BF16),
                   jax.ShapeDtypeStruct((num_seqs, seq_len, 1), F32)],
        scratch_shapes=[pltpu.VMEM((pairs, num_seqs, seq_len, LANES), BF16)] * 3
        + [pltpu.VMEM((num_seqs, seq_len, inner), BF16)],
        compiler_params=pltpu.CompilerParams(dimension_semantics=("arbitrary", "arbitrary"), vmem_limit_bytes=60 << 20),
        cost_estimate=pl.CostEstimate(flops=flops, bytes_accessed=32 << 20, transcendentals=num_seqs * num_heads * seq_len * seq_len),
        name="attn",
    )(x, mask, rel_bias, gains, gains, wq, wk, wv, wo, wr, e_col)


def pack_kernel(pos_ref, b_ref, out_ref):
    rows, _ = out_ref.shape
    first = pl.program_id(0) * rows
    acc = None
    for blk in range(b_ref.shape[0]):
        want = lax.broadcasted_iota(jnp.int32, (rows, b_ref.shape[1]), 0) + first
        hot = (want == pos_ref[blk]).astype(F32).astype(BF16)
        part = jnp.dot(hot, b_ref[blk], preferred_element_type=F32)
        acc = part if acc is None else acc + part
    out_ref[...] = acc.astype(BF16)


def pack(layer, pos_row, b, slots, rows=256):
    num_seqs, seq_len, model_dim = b.shape
    return pl.pallas_call(
        pack_kernel,
        grid=(slots // rows,),
        in_specs=[pl.BlockSpec((None, num_seqs, 1, seq_len), lambda i: (layer, 0, 0, 0)),
                  pl.BlockSpec((num_seqs, seq_len, model_dim), lambda i: (0, 0, 0))],
        out_specs=pl.BlockSpec((rows, model_dim), lambda i: (i, 0)),
        out_shape=jax.ShapeDtypeStruct((slots, model_dim), BF16),
        compiler_params=pltpu.CompilerParams(dimension_semantics=("arbitrary",), vmem_limit_bytes=60 << 20),
        cost_estimate=pl.CostEstimate(flops=2 * slots * num_seqs * seq_len * model_dim, bytes_accessed=8 << 20, transcendentals=0),
        name="pack",
    )(pos_row, b)


def combine_kernel(pos_ref, gate_ref, h1_ref, u_ref, out_ref):
    hot = lax.broadcasted_iota(jnp.int32, (h1_ref.shape[0], u_ref.shape[0]), 1) == pos_ref[...]
    u = jnp.dot(hot.astype(F32).astype(BF16), u_ref[...], preferred_element_type=F32)
    out_ref[...] = (h1_ref[...].astype(F32) + gate_ref[...] * u).astype(BF16)


def combine(layer, pos_col, gate, h1, u, rows=256):
    num_seqs, seq_len, model_dim = h1.shape
    slots = u.shape[0]
    tok = lambda last: pl.BlockSpec((None, rows, last), lambda s, i: (s, i, 0))
    return pl.pallas_call(
        combine_kernel,
        grid=(num_seqs, seq_len // rows),
        in_specs=[pl.BlockSpec((None, None, rows, 1), lambda s, i: (layer, s, i, 0)), tok(1), tok(model_dim),
                  pl.BlockSpec((slots, model_dim), lambda s, i: (0, 0))],
        out_specs=tok(model_dim),
        out_shape=jax.ShapeDtypeStruct(h1.shape, BF16),
        compiler_params=pltpu.CompilerParams(dimension_semantics=("arbitrary", "arbitrary"), vmem_limit_bytes=60 << 20),
        cost_estimate=pl.CostEstimate(flops=2 * slots * num_seqs * seq_len * model_dim, bytes_accessed=10 << 20, transcendentals=0),
        name="combine",
    )(pos_col, gate, h1, u)


def ffn_kernel(x_ref, w_in_ref, w_out_ref, y_ref, acc_ref):
    part = pl.program_id(1)
    act = jnp.maximum(jnp.dot(x_ref[...], w_in_ref[...], preferred_element_type=F32), 0.0).astype(BF16)
    down = jnp.dot(act, w_out_ref[...], preferred_element_type=F32)

    @pl.when(part == 0)
    def _():
        acc_ref[...] = down

    @pl.when((part > 0) & (part < pl.num_programs(1) - 1))
    def _():
        acc_ref[...] += down

    @pl.when(part == pl.num_programs(1) - 1)
    def _():
        y_ref[...] = (acc_ref[...] + down).astype(BF16)


def expert_ffn(layer, x, w_in, w_out, cols=768):
    mine, rows, model_dim = x.shape
    ff = w_in.shape[3]
    return pl.pallas_call(
        ffn_kernel,
        grid=(mine, ff // cols),
        in_specs=[pl.BlockSpec((None, rows, model_dim), lambda e, f: (e, 0, 0)),
                  pl.BlockSpec((None, None, model_dim, cols), lambda e, f: (layer, e, 0, f)),
                  pl.BlockSpec((None, None, cols, model_dim), lambda e, f: (layer, e, f, 0))],
        out_specs=pl.BlockSpec((None, rows, model_dim), lambda e, f: (e, 0, 0)),
        out_shape=jax.ShapeDtypeStruct(x.shape, BF16),
        scratch_shapes=[pltpu.VMEM((rows, model_dim), F32)],
        compiler_params=pltpu.CompilerParams(dimension_semantics=("arbitrary", "arbitrary"), vmem_limit_bytes=60 << 20),
        cost_estimate=pl.CostEstimate(flops=4 * mine * rows * model_dim * ff, bytes_accessed=48 << 20, transcendentals=0),
        name="ffn",
    )(x, w_in, w_out)


def solution(mesh):
    token_spec = P(('dp', 'ep'))
    peers = mesh.shape['ep']

    def per_device(x_in, pad_mask, rel_bias, expert_idx, norm_scale, w_query, w_key, w_value, w_attn_out, w_router, w_in, w_out):
        num_seqs, seq_len, model_dim = x_in.shape
        tok_count = num_seqs * seq_len
        layers = w_router.shape[0]
        num_experts = w_router.shape[2]
        mine = num_experts // peers
        capacity = (CAP_FACTOR * tok_count + num_experts - 1) // num_experts
        slots = num_experts * capacity
        expert_ids = jnp.arange(num_experts, dtype=jnp.int32)
        base = ((expert_ids % mine) * (peers * capacity) + (expert_ids // mine) * capacity).astype(F32)
        blocks = expert_idx.reshape(layers, tok_count // LANES, LANES)
        pos = pl.pallas_call(
            functools.partial(slots_kernel, capacity, slots),
            out_shape=jax.ShapeDtypeStruct(blocks.shape, jnp.int32),
            name="slots",
        )(blocks, base.reshape(1, num_experts, 1))
        pos_row = pos.reshape(layers, num_seqs, 1, seq_len)
        pos_col = pos.reshape(layers, num_seqs, seq_len, 1)
        e_col = expert_idx.reshape(layers, num_seqs, seq_len, 1)
        mask = pad_mask.reshape(num_seqs, 1, seq_len)
        gains = norm_scale.reshape(layers * 2, 1, model_dim)
        hidden = x_in
        for layer in range(layers):
            h1, b, gate = attention(layer, hidden, mask, rel_bias, gains, w_query, w_key, w_value, w_attn_out, w_router, e_col)
            packed = pack(layer, pos_row, b, slots)
            received = lax.all_to_all(packed.reshape(mine, peers, capacity, model_dim), 'ep', 1, 1, tiled=True)
            rows = expert_ffn(layer, received.reshape(mine, peers * capacity, model_dim), w_in, w_out)
            returned = lax.all_to_all(rows.reshape(mine, peers, capacity, model_dim), 'ep', 1, 1, tiled=True)
            hidden = combine(layer, pos_col, gate, h1, returned.reshape(slots, model_dim))
        return hidden

    return jax.shard_map(per_device, mesh=mesh, in_specs=(token_spec, token_spec, P(), P(None, ('dp', 'ep')), P(), P(), P(), P(), P(), P(), P(None, 'ep'), P(None, 'ep')), out_specs=token_spec, check_vma=False)
```

time: 894 us -> 721 us (0.81); the launches traced: 884 us -> 720 us
  Pallas kernels: 0 us -> 230 us
  matrix products: 219 us -> 0 us
  local copies, waits for them, and re-layouts: 193 us -> 38.4 us
  other arithmetic: 140 us -> 0.63 us
  blocking collectives: 233 us -> 344 us
  waiting for transfers between devices: 88.1 us -> 102 us
    pallas_call x0 -> x9, Pallas kernels: none -> 230 us  [the longest x2 97.8 us: attention(): pl.pallas_call(functools.partial(attn_kernel, head_dim), grid=(pairs, num...]
    dot_general x16 -> x0, matrix products: 173 us -> none  [the longest x2 49.5 us: expert_ffn(): jnp.einsum('ecf,efd->ecd', inner_act, down_w, preferred_element_type=jnp....]
    all_to_all x2 -> x3, blocking collectives: 233 us -> 344 us  [the longest x2 234 us: per_device(): lax.all_to_all(packed.reshape(mine, peers, capacity, model_dim), 'ep', 1,...]
    gather x16 -> x0, local copies, waits for them, and re-layouts: 94.3 us -> none  [the longest x2 27.1 us: dispatch(): jnp.take(normed32.astype(jnp.bfloat16), slot_token, axis=0, mode='fill',...]
    sub x4 -> x0, other arithmetic: 71.9 us -> none  [the longest x2 71.9 us: token_slots(): jnp.arange(tok_count, dtype=jnp.int32) - starts[expert_ids[sort_order]]]
    sub x2 -> x0, matrix products: 45.7 us -> none  [attention(): attn_probs = jax.nn.softmax(scores, axis=-1).astype(jnp.bfloat16)]
    convert_element_type x8 -> x0, local copies, waits for them, and re-layouts: 39.6 us -> none  [the longest x6 23.3 us: project(): out_rows.astype(jnp.bfloat16)]
    scatter x4 -> x0, local copies, waits for them, and re-layouts: 24.9 us -> none  [the longest x2 12.5 us: dispatch(): jnp.full((num_experts * capacity,), tok_count, jnp.int32).at[flat_slot]]
  transfers between devices with their start and end apart: 2 -> 1, of which waited for: 2 -> 1; matrix products, arithmetic and copies ran while one was open for 14% -> 0% of each run, Pallas kernels for 0% -> 0%
where the time goes in v1:
time: 721 us; the launch traced here: 720 us
  blocking collectives  344 us (48%)
  Pallas kernels  230 us (32%)
  waiting for transfers between devices  102 us (14%)
  local copies, waits for them, and re-layouts  38.4 us (5%)
    all_to_all x2, blocking collectives, per_device(): lax.all_to_all(packed.reshape(mine, peers, capacity, model_dim), 'ep', 1,...  234 us
    all_to_all x1, blocking collectives, per_device(): lax.all_to_all(rows.reshape(mine, peers, capacity, model_dim), 'ep', 1, 1...  111 us
    all_to_all x1, waiting for transfers between devices, per_device(): lax.all_to_all(rows.reshape(mine, peers, capacity, model_dim), 'ep', 1, 1...  102 us
    pallas_call x2, Pallas kernels, attention(): pl.pallas_call(functools.partial(attn_kernel, head_dim), grid=(pairs, num...  97.8 us
    pallas_call x2, Pallas kernels, expert_ffn(): pl.pallas_call(ffn_kernel, grid=(mine, ff // cols), in_specs=[pl.BlockSpe...  81.6 us
    pallas_call x2, Pallas kernels, combine(): pl.pallas_call(combine_kernel, grid=(num_seqs, seq_len // rows), in_specs...  24.4 us
    pallas_call x2, Pallas kernels, pack(): pl.pallas_call(pack_kernel, grid=(slots // rows,), in_specs=[pl.BlockSpec...  24.2 us
  transfers between devices with their start and end apart: 1, of which 1 were waited for; matrix products, arithmetic and copies ran while one was open for 0% of the time, Pallas kernels for 0%

profile of v1, /device:TPU:21, one launch (start us, length us, event | category | flops | bytes accessed | tf_op | source)
XLA Modules:
  0.0 720.2 jit_solution(7285891095572622034)
XLA Ops:
  1.3 2.5 copy.46.e_ref
  3.8 2.2 copy.45.wr_ref
  12.5 48.9 %attn.2 = (bf16[3,512,768]{2,1,0:T(8,128)(2,1)}, bf16[3,512,768]{2,1,0:T(8,128)(2,1)}, f32[3,512,1]{2,1,0:T(8,128)}) custom-call(bf16[3,512,768]{2,1,0:T(8,128)(2,1)} %x_ref.1, s32[3,1,512]{2,1,0:T(1,128)} %reshape.106.mask_ref, f32[12,512,512]{2,1,0:T(8,128)} %bias_ref.3, f32[4,1,768]{2,1,0:T(1,128)} %reshape.107.g0_ref.g1_ref, ...), custom_call_target="tpu_custom_call" | custom-call | flops 9663676416 | bytes 33554432 | tf_op jit(solution)/shard_map/attn/pallas_call | solution.py:96
  61.4 12.1 %pack.2 = bf16[3072,768]{1,0:T(8,128)(2,1)} custom-call(s32[2,3,1,512]{3,2,1,0:T(1,128)} %reshape.119.pos_ref, bf16[3,512,768]{2,1,0:T(8,128)(2,1)} %get-tuple-element.13.b_ref), custom_call_target="tpu_custom_call" | custom-call | flops 7247757312 | bytes 8388608 | tf_op jit(solution)/shard_map/pack/pallas_call | solution.py:128
  73.5 2.8 copy.48
  76.3 117.5 %all_to_all.20 = bf16[4,16,48,768]{3,2,0,1:T(8,128)(2,1)S(1)} all-to-all(bf16[4,16,48,768]{3,2,0,1:T(8,128)(2,1)S(1)} %copy.48), channel_id=1, replica_groups=mesh['dp'=4,'ep'=16] {'ep'}, dimensions={1} | all-to-all | bytes 9437184 | tf_op jit(solution)/shard_map/all_to_all | solution.py:229
  193.8 2.5 copy.49
  196.4 40.7 %ffn.2 = bf16[4,768,768]{2,1,0:T(8,128)(2,1)} custom-call(bf16[4,768,768]{2,1,0:T(8,128)(2,1)} %bitcast.13, bf16[2,4,768,3072]{3,2,1,0:T(8,128)(2,1)} %w_in_ref.3, bf16[2,4,3072,768]{3,2,1,0:T(8,128)(2,1)} %w_out_ref.3), custom_call_target="tpu_custom_call" | custom-call | flops 28991029248 | bytes 50331648 | tf_op jit(solution)/shard_map/ffn/pallas_call | solution.py:185
  237.1 5.0 copy.50
  242.1 5.0 all-to-all-start.1
  247.1 2.6 reshape.118.pos_ref
  249.7 101.8 %all-to-all-done.1 = bf16[4,16,48,768]{3,2,0,1:T(8,128)(2,1)} async-done(((bf16[4,16,48,768]{3,2,0,1:T(8,128)(2,1)}), bf16[4,16,48,768]{3,2,0,1:T(8,128)(2,1)}, u32[]{:S(2)}, u32[]{:S(2)}) %all-to-all-start.1) | async-done | bytes 4718624 | tf_op jit(solution)/shard_map/all_to_all | solution.py:231
  351.5 4.9 copy.51
  356.4 12.3 %combine.2.x_ref = bf16[3,512,768]{2,1,0:T(8,128)(2,1)} custom-call(s32[2,3,512,1]{3,2,1,0:T(8,128)} %reshape.118.pos_ref, f32[3,512,1]{2,1,0:T(8,128)} %get-tuple-element.11.gate_ref, bf16[3,512,768]{2,1,0:T(8,128)(2,1)} %get-tuple-element.12.h1_ref, bf16[3072,768]{1,0:T(8,128)(2,1)} %bitcast.10), custom_call_target="tpu_custom_call" | custom-call | flops 7247757312 | bytes 10485760 | tf_op jit(solution)/shard_map/combine/pallas_call | solution.py:151
  368.7 49.0 %attn.3 = (bf16[3,512,768]{2,1,0:T(8,128)(2,1)}, bf16[3,512,768]{2,1,0:T(8,128)(2,1)}, f32[3,512,1]{2,1,0:T(8,128)}) custom-call(bf16[3,512,768]{2,1,0:T(8,128)(2,1)} %combine.2.x_ref, s32[3,1,512]{2,1,0:T(1,128)} %reshape.106.mask_ref, f32[12,512,512]{2,1,0:T(8,128)} %bias_ref.3, f32[4,1,768]{2,1,0:T(1,128)} %reshape.107.g0_ref.g1_ref, ...), custom_call_target="tpu_custom_call" | custom-call | flops 9663676416 | bytes 33554432 | tf_op jit(solution)/shard_map/attn/pallas_call | solution.py:96
  417.6 12.1 %pack.3 = bf16[3072,768]{1,0:T(8,128)(2,1)} custom-call(s32[2,3,1,512]{3,2,1,0:T(1,128)} %reshape.119.pos_ref, bf16[3,512,768]{2,1,0:T(8,128)(2,1)} %get-tuple-element.16.b_ref), custom_call_target="tpu_custom_call" | custom-call | flops 7247757312 | bytes 8388608 | tf_op jit(solution)/shard_map/pack/pallas_call | solution.py:128
  429.7 2.8 copy.56
  432.5 116.3 %all_to_all.21 = bf16[4,16,48,768]{3,2,0,1:T(8,128)(2,1)S(1)} all-to-all(bf16[4,16,48,768]{3,2,0,1:T(8,128)(2,1)S(1)} %copy.56), channel_id=1, replica_groups=mesh['dp'=4,'ep'=16] {'ep'}, dimensions={1} | all-to-all | bytes 9437184 | tf_op jit(solution)/shard_map/all_to_all | solution.py:229
  548.8 2.5 copy.57
  551.3 40.8 %ffn.3 = bf16[4,768,768]{2,1,0:T(8,128)(2,1)} custom-call(bf16[4,768,768]{2,1,0:T(8,128)(2,1)} %bitcast.15, bf16[2,4,768,3072]{3,2,1,0:T(8,128)(2,1)} %w_in_ref.3, bf16[2,4,3072,768]{3,2,1,0:T(8,128)(2,1)} %w_out_ref.3), custom_call_target="tpu_custom_call" | custom-call | flops 28991029248 | bytes 50331648 | tf_op jit(solution)/shard_map/ffn/pallas_call | solution.py:185
  592.2 2.8 copy.58
  595.0 110.6 %all_to_all.22 = bf16[4,16,48,768]{3,2,0,1:T(8,128)(2,1)S(1)} all-to-all(bf16[4,16,48,768]{3,2,0,1:T(8,128)(2,1)S(1)} %copy.58), channel_id=1, replica_groups=mesh['dp'=4,'ep'=16] {'ep'}, dimensions={1} | all-to-all | bytes 9437184 | tf_op jit(solution)/shard_map/all_to_all | solution.py:231
  705.6 2.5 copy.59
  708.1 12.2 %combine.3 = bf16[3,512,768]{2,1,0:T(8,128)(2,1)} custom-call(s32[2,3,512,1]{3,2,1,0:T(8,128)} %reshape.118.pos_ref, f32[3,512,1]{2,1,0:T(8,128)} %get-tuple-element.14.gate_ref, bf16[3,512,768]{2,1,0:T(8,128)(2,1)} %get-tuple-element.15.h1_ref, bf16[3072,768]{1,0:T(8,128)(2,1)} %bitcast.9), custom_call_target="tpu_custom_call" | custom-call | flops 7247757312 | bytes 10485760 | tf_op jit(solution)/shard_map/combine/pallas_call | solution.py:151
  (9 shorter events, 7.9 us)
Async XLA Ops:
  242.1 5.0 copy-start
  242.1 109.4 %all-to-all-start.1 = ((bf16[4,16,48,768]{3,2,0,1:T(8,128)(2,1)}), bf16[4,16,48,768]{3,2,0,1:T(8,128)(2,1)}, u32[]{:S(2)}, u32[]{:S(2)}) async-start(bf16[4,16,48,768]{3,2,0,1:T(8,128)(2,1)} %copy.50), calls=%async_computation.1 | async-start | bytes 9437184 | tf_op jit(solution)/shard_map/all_to_all | solution.py:231

commit v2 on v1

--- a/solution.py
+++ b/solution.py
@@ -111,90 +111,131 @@
     )(x, mask, rel_bias, gains, gains, wq, wk, wv, wo, wr, e_col)
 
 
-def pack_kernel(pos_ref, b_ref, out_ref):
-    rows, _ = out_ref.shape
-    first = pl.program_id(0) * rows
-    acc = None
-    for blk in range(b_ref.shape[0]):
-        want = lax.broadcasted_iota(jnp.int32, (rows, b_ref.shape[1]), 0) + first
-        hot = (want == pos_ref[blk]).astype(F32).astype(BF16)
-        part = jnp.dot(hot, b_ref[blk], preferred_element_type=F32)
-        acc = part if acc is None else acc + part
-    out_ref[...] = acc.astype(BF16)
-
-
-def pack(layer, pos_row, b, slots, rows=256):
-    num_seqs, seq_len, model_dim = b.shape
+def moe_kernel(layer, axis, pos_row_ref, pos_col_ref, gate_ref, h1_ref, b_ref, w_in_ref, w_out_ref, out_ref,
+               packed, recv, ret, w_in_buf, w_out_buf, acc, u_acc, out_send, out_recv, back_send, back_recv, w_sem):
+    mine, peers, capacity, dim = packed.shape
+    num_seqs, seq_len, _ = b_ref.shape
+    ff = w_in_buf.shape[2]
+    rows = peers * capacity
+    me = lax.axis_index(axis)
+    other = lambda shift: lax.rem(me + shift, peers)
+
+    def weights(k):
+        slot = lax.rem(k, 2)
+        return (pltpu.make_async_copy(w_in_ref.at[layer, k], w_in_buf.at[slot], w_sem.at[0, slot]),
+                pltpu.make_async_copy(w_out_ref.at[layer, k], w_out_buf.at[slot], w_sem.at[1, slot]))
+
+    def there(k, peer, slot):
+        return pltpu.make_async_remote_copy(
+            src_ref=packed.at[k, peer], dst_ref=recv.at[k, slot], send_sem=out_send.at[k, peer],
+            recv_sem=out_recv.at[k, slot], device_id={axis: peer}, device_id_type=pl.DeviceIdType.MESH)
+
+    def back(k, peer, slot):
+        return pltpu.make_async_remote_copy(
+            src_ref=recv.at[k, peer], dst_ref=ret.at[k, slot], send_sem=back_send.at[k, peer],
+            recv_sem=back_recv.at[k, slot], device_id={axis: peer}, device_id_type=pl.DeviceIdType.MESH)
+
+    def each_peer(fn):
+        @pl.loop(1, peers)
+        def _(shift):
+            fn(other(shift))
+
+    for k in range(min(2, mine)):
+        for copy in weights(k):
+            copy.start()
+
+    barrier = pltpu.get_barrier_semaphore()
+    each_peer(lambda peer: pl.semaphore_signal(barrier, inc=1, device_id={axis: peer}, device_id_type=pl.DeviceIdType.MESH))
+    pl.semaphore_wait(barrier, peers - 1)
+
+    half = peers // 2
+    @pl.loop(0, mine)
+    def _(k):
+        @pl.loop(0, 2)
+        def _(part):
+            first = k * rows + part * (half * capacity)
+            want = lax.broadcasted_iota(jnp.int32, (half * capacity, seq_len), 0) + first
+            total = None
+            for s in range(num_seqs):
+                hot = (want == pos_row_ref[layer, s]).astype(F32).astype(BF16)
+                term = jnp.dot(hot, b_ref[s], preferred_element_type=F32)
+                total = term if total is None else total + term
+            packed[k, pl.ds(part * half, half)] = total.astype(BF16).reshape(half, capacity, dim)
+        each_peer(lambda peer: there(k, peer, me).start())
+        recv[k, me] = packed[k, me]
+
+    u_acc[...] = jnp.zeros_like(u_acc)
+
+    @pl.loop(0, mine)
+    def _(k):
+        slot = lax.rem(k, 2)
+        for copy in weights(k):
+            copy.wait()
+        each_peer(lambda peer: there(k, peer, peer).wait_recv())
+        acc[...] = jnp.zeros_like(acc)
+
+        @pl.loop(0, ff // dim)
+        def _(part):
+            cols = pl.ds(pl.multiple_of(part * dim, dim), dim)
+            act = jnp.dot(recv[k].reshape(rows, dim), w_in_buf[slot, :, cols], preferred_element_type=F32)
+            act = jnp.maximum(act, 0.0).astype(BF16)
+            acc[...] += jnp.dot(act, w_out_buf[slot, cols, :], preferred_element_type=F32)
+
+        recv[k] = acc[...].astype(BF16).reshape(peers, capacity, dim)
+        each_peer(lambda peer: back(k, peer, me).start())
+        ret[k, me] = recv[k, me]
+
+        @pl.when(k + 2 < mine)
+        def _():
+            for copy in weights(k + 2):
+                copy.start()
+
+    def gather_back(k, last):
+        each_peer(lambda peer: back(k, peer, peer).wait_recv())
+        for s in range(num_seqs):
+            @pl.loop(0, seq_len // 256)
+            def _(part):
+                tok = pl.ds(pl.multiple_of(part * 256, 256), 256)
+                want = lax.broadcasted_iota(jnp.int32, (256, rows), 1) + k * rows
+                hot = (want == pos_col_ref[layer, s, tok, :]).astype(F32).astype(BF16)
+                u = jnp.dot(hot, ret[k].reshape(rows, dim), preferred_element_type=F32) + u_acc[s, tok, :].astype(F32)
+                if last:
+                    out_ref[s, tok, :] = (h1_ref[s, tok, :].astype(F32) + gate_ref[s, tok, :] * u).astype(BF16)
+                else:
+                    u_acc[s, tok, :] = u.astype(BF16)
+
+    @pl.loop(0, mine - 1)
+    def _(k):
+        gather_back(k, False)
+
+    gather_back(mine - 1, True)
+
+    @pl.loop(0, mine)
+    def _(k):
+        each_peer(lambda peer: there(k, peer, me).wait_send())
+        each_peer(lambda peer: back(k, peer, me).wait_send())
+
+
+def moe(layer, axis, peers, capacity, pos_row, pos_col, gate, h1, b, w_in, w_out):
+    num_seqs, seq_len, dim = h1.shape
+    mine, _, ff = w_in.shape[1:]
+    rows = peers * capacity
+    near = pl.BlockSpec(memory_space=pltpu.VMEM)
+    hbm = pl.BlockSpec(memory_space=pl.ANY)
+    buffer = pltpu.VMEM((mine, peers, capacity, dim), BF16)
+    sems = pltpu.SemaphoreType.DMA((mine, peers))
     return pl.pallas_call(
-        pack_kernel,
-        grid=(slots // rows,),
-        in_specs=[pl.BlockSpec((None, num_seqs, 1, seq_len), lambda i: (layer, 0, 0, 0)),
-                  pl.BlockSpec((num_seqs, seq_len, model_dim), lambda i: (0, 0, 0))],
-        out_specs=pl.BlockSpec((rows, model_dim), lambda i: (i, 0)),
-        out_shape=jax.ShapeDtypeStruct((slots, model_dim), BF16),
-        compiler_params=pltpu.CompilerParams(dimension_semantics=("arbitrary",), vmem_limit_bytes=60 << 20),
-        cost_estimate=pl.CostEstimate(flops=2 * slots * num_seqs * seq_len * model_dim, bytes_accessed=8 << 20, transcendentals=0),
-        name="pack",
-    )(pos_row, b)
-
-
-def combine_kernel(pos_ref, gate_ref, h1_ref, u_ref, out_ref):
-    hot = lax.broadcasted_iota(jnp.int32, (h1_ref.shape[0], u_ref.shape[0]), 1) == pos_ref[...]
-    u = jnp.dot(hot.astype(F32).astype(BF16), u_ref[...], preferred_element_type=F32)
-    out_ref[...] = (h1_ref[...].astype(F32) + gate_ref[...] * u).astype(BF16)
-
-
-def combine(layer, pos_col, gate, h1, u, rows=256):
-    num_seqs, seq_len, model_dim = h1.shape
-    slots = u.shape[0]
-    tok = lambda last: pl.BlockSpec((None, rows, last), lambda s, i: (s, i, 0))
-    return pl.pallas_call(
-        combine_kernel,
-        grid=(num_seqs, seq_len // rows),
-        in_specs=[pl.BlockSpec((None, None, rows, 1), lambda s, i: (layer, s, i, 0)), tok(1), tok(model_dim),
-                  pl.BlockSpec((slots, model_dim), lambda s, i: (0, 0))],
-        out_specs=tok(model_dim),
+        functools.partial(moe_kernel, layer, axis),
+        in_specs=[near] * 5 + [hbm, hbm],
+        out_specs=near,
         out_shape=jax.ShapeDtypeStruct(h1.shape, BF16),
-        compiler_params=pltpu.CompilerParams(dimension_semantics=("arbitrary", "arbitrary"), vmem_limit_bytes=60 << 20),
-        cost_estimate=pl.CostEstimate(flops=2 * slots * num_seqs * seq_len * model_dim, bytes_accessed=10 << 20, transcendentals=0),
-        name="combine",
-    )(pos_col, gate, h1, u)
-
-
-def ffn_kernel(x_ref, w_in_ref, w_out_ref, y_ref, acc_ref):
-    part = pl.program_id(1)
-    act = jnp.maximum(jnp.dot(x_ref[...], w_in_ref[...], preferred_element_type=F32), 0.0).astype(BF16)
-    down = jnp.dot(act, w_out_ref[...], preferred_element_type=F32)
-
-    @pl.when(part == 0)
-    def _():
-        acc_ref[...] = down
-
-    @pl.when((part > 0) & (part < pl.num_programs(1) - 1))
-    def _():
-        acc_ref[...] += down
-
-    @pl.when(part == pl.num_programs(1) - 1)
-    def _():
-        y_ref[...] = (acc_ref[...] + down).astype(BF16)
-
-
-def expert_ffn(layer, x, w_in, w_out, cols=768):
-    mine, rows, model_dim = x.shape
-    ff = w_in.shape[3]
-    return pl.pallas_call(
-        ffn_kernel,
-        grid=(mine, ff // cols),
-        in_specs=[pl.BlockSpec((None, rows, model_dim), lambda e, f: (e, 0, 0)),
-                  pl.BlockSpec((None, None, model_dim, cols), lambda e, f: (layer, e, 0, f)),
-                  pl.BlockSpec((None, None, cols, model_dim), lambda e, f: (layer, e, f, 0))],
-        out_specs=pl.BlockSpec((None, rows, model_dim), lambda e, f: (e, 0, 0)),
-        out_shape=jax.ShapeDtypeStruct(x.shape, BF16),
-        scratch_shapes=[pltpu.VMEM((rows, model_dim), F32)],
-        compiler_params=pltpu.CompilerParams(dimension_semantics=("arbitrary", "arbitrary"), vmem_limit_bytes=60 << 20),
-        cost_estimate=pl.CostEstimate(flops=4 * mine * rows * model_dim * ff, bytes_accessed=48 << 20, transcendentals=0),
-        name="ffn",
-    )(x, w_in, w_out)
+        scratch_shapes=[buffer, buffer, buffer, pltpu.VMEM((2, dim, ff), BF16), pltpu.VMEM((2, ff, dim), BF16),
+                        pltpu.VMEM((rows, dim), F32), pltpu.VMEM((num_seqs, seq_len, dim), BF16),
+                        sems, sems, sems, sems, pltpu.SemaphoreType.DMA((2, 2))],
+        compiler_params=pltpu.CompilerParams(collective_id=layer, has_side_effects=True, vmem_limit_bytes=67043328),
+        cost_estimate=pl.CostEstimate(flops=4 * mine * rows * dim * ff, bytes_accessed=48 << 20, transcendentals=0),
+        name="moe",
+    )(pos_row, pos_col, gate, h1, b, w_in, w_out)
 
 
 def solution(mesh):
@@ -225,11 +266,7 @@
         hidden = x_in
         for layer in range(layers):
             h1, b, gate = attention(layer, hidden, mask, rel_bias, gains, w_query, w_key, w_value, w_attn_out, w_router, e_col)
-            packed = pack(layer, pos_row, b, slots)
-            received = lax.all_to_all(packed.reshape(mine, peers, capacity, model_dim), 'ep', 1, 1, tiled=True)
-            rows = expert_ffn(layer, received.reshape(mine, peers * capacity, model_dim), w_in, w_out)
-            returned = lax.all_to_all(rows.reshape(mine, peers, capacity, model_dim), 'ep', 1, 1, tiled=True)
-            hidden = combine(layer, pos_col, gate, h1, returned.reshape(slots, model_dim))
+            hidden = moe(layer, 'ep', peers, capacity, pos_row, pos_col, gate, h1, b, w_in, w_out)
         return hidden
 
     return jax.shard_map(per_device, mesh=mesh, in_specs=(token_spec, token_spec, P(), P(None, ('dp', 'ep')), P(), P(), P(), P(), P(), P(), P(None, 'ep'), P(None, 'ep')), out_specs=token_spec, check_vma=False)

time: 721 us -> 574 us (0.80)
  blocking collectives: 344 us -> 0 us
  Pallas kernels: 230 us -> 557 us
  waiting for transfers between devices: 102 us -> 0 us
  local copies, waits for them, and re-layouts: 38.4 us -> 15.7 us
    all_to_all x3 -> x0, blocking collectives: 344 us -> none  [the longest x2 234 us: per_device(): lax.all_to_all(packed.reshape(mine, peers, capacity, model_dim), 'ep', 1,...]
    pallas_call x6 -> x2, Pallas kernels: 130 us -> 457 us  [moe(): pl.pallas_call(functools.partial(moe_kernel, layer, axis), in_specs=[near...]
    all_to_all x1 -> x0, waiting for transfers between devices: 102 us -> none  [per_device(): lax.all_to_all(rows.reshape(mine, peers, capacity, model_dim), 'ep', 1, 1...]
    reshape x4 -> x0, local copies, waits for them, and re-layouts: 13.4 us -> none  [the longest x2 7.83 us: per_device(): rows.reshape(mine, peers, capacity, model_dim)]
    all_to_all x4 -> x0, local copies, waits for them, and re-layouts: 12.4 us -> none  [the longest x2 7.4 us: per_device(): lax.all_to_all(rows.reshape(mine, peers, capacity, model_dim), 'ep', 1, 1...]
  transfers between devices with their start and end apart: 1 -> 0, of which waited for: 1 -> 0; matrix products, arithmetic and copies ran while one was open for 0% -> 0% of each run, Pallas kernels for 0% -> 0%
where the time goes in v2:
time: 574 us
  Pallas kernels  557 us (97%)
  local copies, waits for them, and re-layouts  15.7 us (3%)
    pallas_call x2, Pallas kernels, moe(): pl.pallas_call(functools.partial(moe_kernel, layer, axis), in_specs=[near...  457 us
    pallas_call x2, Pallas kernels, attention(): pl.pallas_call(functools.partial(attn_kernel, head_dim), grid=(pairs, num...  98.2 us

profile of v2, /device:TPU:21, one launch (start us, length us, event | category | flops | bytes accessed | tf_op | source)
XLA Modules:
  0.0 573.7 jit_solution(13300479978977118296)
XLA Ops:
  0.0 0.0 copy-start
  0.0 1.3 reshape.83.mask_ref
  1.3 1.3 reshape.84.g0_ref.g1_ref
  2.6 0.7 copy.26
  3.3 0.6 reshape.80.e_ref
  4.0 0.6 fusion.8.base_ref
  4.6 1.9 slots.1
  6.5 1.3 reshape.86.pos_row_ref
  7.9 2.2 copy.28.wr_ref
  10.1 3.3 reshape.87.pos_col_ref
  13.4 0.0 copy-done
  13.4 1.7 copy.29.e_ref
  15.1 49.0 %attn.2 = (bf16[3,512,768]{2,1,0:T(8,128)(2,1)}, bf16[3,512,768]{2,1,0:T(8,128)(2,1)}, f32[3,512,1]{2,1,0:T(8,128)}) custom-call(bf16[3,512,768]{2,1,0:T(8,128)(2,1)} %x_ref.1, s32[3,1,512]{2,1,0:T(1,128)} %reshape.83.mask_ref, f32[12,512,512]{2,1,0:T(8,128)} %bias_ref.3, f32[4,1,768]{2,1,0:T(1,128)} %reshape.84.g0_ref.g1_ref, ...), custom_call_target="tpu_custom_call" | custom-call | flops 9663676416 | bytes 33554432 | tf_op jit(solution)/shard_map/attn/pallas_call | solution.py:96
  64.0 231.7 %moe.2.x_ref = bf16[3,512,768]{2,1,0:T(8,128)(2,1)} custom-call(s32[2,3,1,512]{3,2,1,0:T(1,128)} %reshape.86.pos_row_ref, s32[2,3,512,1]{3,2,1,0:T(8,128)} %reshape.87.pos_col_ref, f32[3,512,1]{2,1,0:T(8,128)} %get-tuple-element.11.gate_ref, bf16[3,512,768]{2,1,0:T(8,128)(2,1)} %get-tuple-element.12.h1_ref, bf16[3,512,768]{2,1,0:T(8,128)(2,1)} %get-tuple-element.13.b_ref, ...), custom_call_target="tpu_custom_call" | custom-call | flops 28991029248 | bytes 50331648 | tf_op jit(solution)/shard_map/moe/pallas_call | solution.py:227
  295.8 49.2 %attn.3 = (bf16[3,512,768]{2,1,0:T(8,128)(2,1)}, bf16[3,512,768]{2,1,0:T(8,128)(2,1)}, f32[3,512,1]{2,1,0:T(8,128)}) custom-call(bf16[3,512,768]{2,1,0:T(8,128)(2,1)} %moe.2.x_ref, s32[3,1,512]{2,1,0:T(1,128)} %reshape.83.mask_ref, f32[12,512,512]{2,1,0:T(8,128)} %bias_ref.3, f32[4,1,768]{2,1,0:T(1,128)} %reshape.84.g0_ref.g1_ref, ...), custom_call_target="tpu_custom_call" | custom-call | flops 9663676416 | bytes 33554432 | tf_op jit(solution)/shard_map/attn/pallas_call | solution.py:96
  345.0 225.4 %moe.3 = bf16[3,512,768]{2,1,0:T(8,128)(2,1)} custom-call(s32[2,3,1,512]{3,2,1,0:T(1,128)} %reshape.86.pos_row_ref, s32[2,3,512,1]{3,2,1,0:T(8,128)} %reshape.87.pos_col_ref, f32[3,512,1]{2,1,0:T(8,128)} %get-tuple-element.14.gate_ref, bf16[3,512,768]{2,1,0:T(8,128)(2,1)} %get-tuple-element.15.h1_ref, bf16[3,512,768]{2,1,0:T(8,128)(2,1)} %get-tuple-element.16.b_ref, ...), custom_call_target="tpu_custom_call" | custom-call | flops 28991029248 | bytes 50331648 | tf_op jit(solution)/shard_map/moe/pallas_call | solution.py:227
  570.4 3.2 copy.37
Async XLA Ops:
  0.0 13.4 %copy-start = (s32[2,3,512]{2,0,1:T(2,128)S(1)}, s32[2,3,512]{2,0,1:T(2,128)}, u32[]{:S(2)}) copy-start(s32[2,3,512]{2,0,1:T(2,128)} %param.15) | copy-start | bytes 36868

commit v3 on v2

v3 whole, which is shorter than its diff:
```python
import functools

import jax
import jax.numpy as jnp
from jax import lax
from jax.experimental import pallas as pl
from jax.experimental.pallas import tpu as pltpu
from jax.sharding import PartitionSpec as P

NORM_EPS = 1e-6
NEG_BIG = -1e9
CAP_FACTOR = 2
LANES = 128
F32 = jnp.float32
BF16 = jnp.bfloat16


def rms(hid32, gain):
    return hid32 * lax.rsqrt(jnp.mean(hid32 * hid32, axis=-1, keepdims=True) + NORM_EPS) * gain


def slots_kernel(capacity, drop, e_ref, base_ref, pos_ref):
    layers, num_seqs, seq_len = e_ref.shape
    num_experts = base_ref.shape[1]
    row = lax.broadcasted_iota(jnp.int32, (LANES, LANES), 0)
    col = lax.broadcasted_iota(jnp.int32, (LANES, LANES), 1)
    upper = (row <= col).astype(F32).astype(BF16)
    experts = lax.broadcasted_iota(jnp.int32, (num_experts, LANES), 0)
    for layer in range(layers):
        carry = jnp.zeros((num_experts, 1), F32)
        for blk in range(num_seqs * seq_len // LANES):
            seq, first = divmod(blk * LANES, seq_len)
            hit = experts == e_ref[layer, seq:seq + 1, first:first + LANES]
            hot = hit.astype(F32)
            cum = jnp.dot(hot.astype(BF16), upper, preferred_element_type=F32) + (carry - 1.0)
            slot = jnp.sum(hot * cum, axis=0, keepdims=True)
            base = jnp.sum(hot * base_ref[0], axis=0, keepdims=True)
            carry = carry + jnp.sum(hot, axis=1, keepdims=True)
            pos_ref[layer, seq:seq + 1, first:first + LANES] = jnp.where(slot < capacity, base + slot, float(drop)).astype(jnp.int32)


def attn_kernel(layer, head_dim, x_ref, mask_ref, bias_ref, gain_ref, wq_ref, wk_ref, wv_ref, wo_ref,
                h1_ref, b_ref, q_s, k_s, v_s, ctx_s):
    pair = pl.program_id(0)
    pairs = pl.num_programs(0)
    n_pairs, num_seqs, _, width = q_s.shape

    @pl.when(pair == 0)
    def _():
        @pl.loop(0, num_seqs)
        def _(seq):
            a = rms(x_ref[seq].astype(F32), gain_ref[layer, 0:1, :]).astype(BF16)
            for w_ref, dst in ((wq_ref, q_s), (wk_ref, k_s), (wv_ref, v_s)):
                rows = jnp.dot(a, w_ref[...], preferred_element_type=F32).astype(BF16)
                for j in range(n_pairs):
                    dst[j, seq] = rows[:, j * width:(j + 1) * width]

    for seq in range(num_seqs):
        q2, k2, v2 = q_s[pair, seq], k_s[pair, seq], v_s[pair, seq]
        lane = lax.broadcasted_iota(jnp.int32, q2.shape, 1)
        mask_row = jnp.where(mask_ref[seq:seq + 1, :] > 0, 0.0, NEG_BIG)
        parts = []
        for half in range(width // head_dim):
            mine = (lane >= half * head_dim) & (lane < (half + 1) * head_dim)
            qh = jnp.where(mine, q2, jnp.zeros_like(q2))
            s = lax.dot_general(qh, k2, (((1,), (1,)), ((), ())), preferred_element_type=F32)
            s = s + bias_ref[half] + mask_row
            p = jnp.exp(s - jnp.max(s, axis=-1, keepdims=True))
            p = (p * (1.0 / jnp.sum(p, axis=-1, keepdims=True))).astype(BF16)
            o = jnp.dot(p, v2, preferred_element_type=F32)
            parts.append(jnp.where(mine, o, 0.0))
        ctx_s[seq, :, pl.ds(pl.multiple_of(pair * width, width), width)] = sum(parts).astype(BF16)

    @pl.when(pair == pairs - 1)
    def _():
        @pl.loop(0, num_seqs)
        def _(seq):
            o = jnp.dot(ctx_s[seq], wo_ref[...], preferred_element_type=F32)
            h1 = (x_ref[seq].astype(F32) + o).astype(BF16)
            h1_ref[seq] = h1
            b_ref[seq] = rms(h1.astype(F32), gain_ref[layer, 1:2, :]).astype(BF16)


def attention(layer, x, mask, rel_bias, gains, wq, wk, wv, wo):
    num_seqs, seq_len, model_dim = x.shape
    num_heads = rel_bias.shape[0]
    inner = wq.shape[2]
    head_dim = inner // num_heads
    per = LANES // head_dim
    pairs = num_heads // per
    full = lambda *shape: pl.BlockSpec(shape, lambda p: (0,) * len(shape))
    of_layer = lambda *shape: pl.BlockSpec((None,) + shape, lambda p: (layer,) + (0,) * len(shape))
    flops = 2 * num_seqs * seq_len * (4 * model_dim * inner + 2 * seq_len * inner)
    return pl.pallas_call(
        functools.partial(attn_kernel, layer, head_dim),
        grid=(pairs,),
        in_specs=[full(num_seqs, seq_len, model_dim), full(num_seqs, seq_len),
                  pl.BlockSpec((per, seq_len, seq_len), lambda p: (p, 0, 0)), full(*gains.shape),
                  of_layer(model_dim, inner), of_layer(model_dim, inner), of_layer(model_dim, inner),
                  of_layer(inner, model_dim)],
        out_specs=[full(num_seqs, seq_len, model_dim), full(num_seqs, seq_len, model_dim)],
        out_shape=[jax.ShapeDtypeStruct(x.shape, BF16), jax.ShapeDtypeStruct(x.shape, BF16)],
        scratch_shapes=[pltpu.VMEM((pairs, num_seqs, seq_len, LANES), BF16)] * 3
        + [pltpu.VMEM((num_seqs, seq_len, inner), BF16)],
        compiler_params=pltpu.CompilerParams(dimension_semantics=("arbitrary",), vmem_limit_bytes=60 << 20),
        cost_estimate=pl.CostEstimate(flops=flops, bytes_accessed=32 << 20, transcendentals=num_seqs * num_heads * seq_len * seq_len),
        name="attn",
    )(x, mask, rel_bias, gains, wq, wk, wv, wo)


def moe_kernel(layer, axis, pos_ref, e_ref, gain_ref, wr_ref, h1_ref, b_ref, w_in_ref, w_out_ref, out_ref,
               packed, recv, ret, w_in_buf, w_out_buf, acc, u_acc, pos_col, gate_col, out_send, out_recv, back_send, back_recv, w_sem):
    mine, peers, capacity, dim = packed.shape
    num_seqs, seq_len, _ = b_ref.shape
    ff = w_in_buf.shape[2]
    rows = peers * capacity
    me = lax.axis_index(axis)
    other = lambda shift: lax.rem(me + shift, peers)

    def weights(k):
        slot = lax.rem(k, 2)
        return (pltpu.make_async_copy(w_in_ref.at[layer, k], w_in_buf.at[slot], w_sem.at[0, slot]),
                pltpu.make_async_copy(w_out_ref.at[layer, k], w_out_buf.at[slot], w_sem.at[1, slot]))

    def there(k, peer, slot):
        return pltpu.make_async_remote_copy(
            src_ref=packed.at[k, peer], dst_ref=recv.at[k, slot], send_sem=out_send.at[k, peer],
            recv_sem=out_recv.at[k, slot], device_id={axis: peer}, device_id_type=pl.DeviceIdType.MESH)

    def back(k, peer, slot):
        return pltpu.make_async_remote_copy(
            src_ref=recv.at[k, peer], dst_ref=ret.at[k, slot], send_sem=back_send.at[k, peer],
            recv_sem=back_recv.at[k, slot], device_id={axis: peer}, device_id_type=pl.DeviceIdType.MESH)

    def each_peer(fn):
        @pl.loop(1, peers)
        def _(shift):
            fn(other(shift))

    for k in range(min(2, mine)):
        for copy in weights(k):
            copy.start()

    barrier = pltpu.get_barrier_semaphore()
    each_peer(lambda peer: pl.semaphore_signal(barrier, inc=1, device_id={axis: peer}, device_id_type=pl.DeviceIdType.MESH))
    pl.semaphore_wait(barrier, peers - 1)

    half = peers // 2
    @pl.loop(0, mine)
    def _(k):
        @pl.loop(0, 2)
        def _(part):
            first = k * rows + part * (half * capacity)
            want = lax.broadcasted_iota(jnp.int32, (half * capacity, seq_len), 0) + first
            total = None
            for s in range(num_seqs):
                hot = (want == pos_ref[layer, s:s + 1, :]).astype(F32).astype(BF16)
                term = jnp.dot(hot, b_ref[s], preferred_element_type=F32)
                total = term if total is None else total + term
            packed[k, pl.ds(part * half, half)] = total.astype(BF16).reshape(half, capacity, dim)
        each_peer(lambda peer: there(k, peer, me).start())
        recv[k, me] = packed[k, me]

    u_acc[...] = jnp.zeros_like(u_acc)
    column = lambda row: jnp.broadcast_to(row, (LANES, row.shape[1])).T[:, :1]
    for s in range(num_seqs):
        @pl.loop(0, seq_len // 256)
        def _(part):
            tok = pl.ds(pl.multiple_of(part * 256, 256), 256)
            pos_col[s, tok, :] = column(pos_ref[layer, s:s + 1, tok].astype(F32)).astype(jnp.int32)
            r = rms(h1_ref[s, tok, :].astype(F32), gain_ref[layer, 1:2, :])
            logits = lax.dot_general(wr_ref[layer], r, (((1,), (1,)), ((), ())),
                                     precision=lax.Precision.HIGHEST, preferred_element_type=F32)
            ex = jnp.exp(logits - jnp.max(logits, axis=0, keepdims=True))
            chosen = lax.broadcasted_iota(jnp.int32, ex.shape, 0) == e_ref[layer, s:s + 1, tok]
            gate = jnp.sum(jnp.where(chosen, ex, 0.0), axis=0, keepdims=True) / jnp.sum(ex, axis=0, keepdims=True)
            gate_col[s, tok, :] = column(gate)

    @pl.loop(0, mine)
    def _(k):
        slot = lax.rem(k, 2)
        for copy in weights(k):
            copy.wait()
        each_peer(lambda peer: there(k, peer, peer).wait_recv())
        acc[...] = jnp.zeros_like(acc)

        @pl.loop(0, ff // dim)
        def _(part):
            cols = pl.ds(pl.multiple_of(part * dim, dim), dim)
            act = jnp.dot(recv[k].reshape(rows, dim), w_in_buf[slot, :, cols], preferred_element_type=F32)
            act = jnp.maximum(act, 0.0).astype(BF16)
            acc[...] += jnp.dot(act, w_out_buf[slot, cols, :], preferred_element_type=F32)

        recv[k] = acc[...].astype(BF16).reshape(peers, capacity, dim)
        each_peer(lambda peer: back(k, peer, me).start())
        ret[k, me] = recv[k, me]

        @pl.when(k + 2 < mine)
        def _():
            for copy in weights(k + 2):
                copy.start()

    def gather_back(k, last):
        each_peer(lambda peer: back(k, peer, peer).wait_recv())
        for s in range(num_seqs):
            @pl.loop(0, seq_len // 256)
            def _(part):
                tok = pl.ds(pl.multiple_of(part * 256, 256), 256)
                want = lax.broadcasted_iota(jnp.int32, (256, rows), 1) + k * rows
                hot = (want == pos_col[s, tok, :]).astype(F32).astype(BF16)
                u = jnp.dot(hot, ret[k].reshape(rows, dim), preferred_element_type=F32) + u_acc[s, tok, :].astype(F32)
                if last:
                    out_ref[s, tok, :] = (h1_ref[s, tok, :].astype(F32) + gate_col[s, tok, :] * u).astype(BF16)
                else:
                    u_acc[s, tok, :] = u.astype(BF16)

    @pl.loop(0, mine - 1)
    def _(k):
        gather_back(k, False)

    gather_back(mine - 1, True)

    @pl.loop(0, mine)
    def _(k):
        each_peer(lambda peer: there(k, peer, me).wait_send())
        each_peer(lambda peer: back(k, peer, me).wait_send())


def moe(layer, axis, peers, capacity, pos, expert_idx, gains, w_router_t, h1, b, w_in, w_out):
    num_seqs, seq_len, dim = h1.shape
    mine, _, ff = w_in.shape[1:]
    rows = peers * capacity
    near = pl.BlockSpec(memory_space=pltpu.VMEM)
    hbm = pl.BlockSpec(memory_space=pl.ANY)
    buffer = pltpu.VMEM((mine, peers, capacity, dim), BF16)
    sems = pltpu.SemaphoreType.DMA((mine, peers))
    return pl.pallas_call(
        functools.partial(moe_kernel, layer, axis),
        in_specs=[near] * 6 + [hbm, hbm],
        out_specs=near,
        out_shape=jax.ShapeDtypeStruct(h1.shape, BF16),
        scratch_shapes=[buffer, buffer, buffer, pltpu.VMEM((2, dim, ff), BF16), pltpu.VMEM((2, ff, dim), BF16),
                        pltpu.VMEM((rows, dim), F32), pltpu.VMEM((num_seqs, seq_len, dim), BF16),
                        pltpu.VMEM((num_seqs, seq_len, 1), jnp.int32), pltpu.VMEM((num_seqs, seq_len, 1), F32),
                        sems, sems, sems, sems, pltpu.SemaphoreType.DMA((2, 2))],
        compiler_params=pltpu.CompilerParams(collective_id=layer, has_side_effects=True, vmem_limit_bytes=67043328),
        cost_estimate=pl.CostEstimate(flops=4 * mine * rows * dim * ff, bytes_accessed=48 << 20, transcendentals=0),
        name="moe",
    )(pos, expert_idx, gains, w_router_t, h1, b, w_in, w_out)


def solution(mesh):
    token_spec = P(('dp', 'ep'))
    peers = mesh.shape['ep']

    def per_device(x_in, pad_mask, rel_bias, expert_idx, norm_scale, w_query, w_key, w_value, w_attn_out, w_router, w_in, w_out):
        num_seqs, seq_len, model_dim = x_in.shape
        tok_count = num_seqs * seq_len
        layers = w_router.shape[0]
        num_experts = w_router.shape[2]
        mine = num_experts // peers
        capacity = (CAP_FACTOR * tok_count + num_experts - 1) // num_experts
        slots = num_experts * capacity
        expert_ids = jnp.arange(num_experts, dtype=jnp.int32)
        base = ((expert_ids % mine) * (peers * capacity) + (expert_ids // mine) * capacity).astype(F32)
        pos = pl.pallas_call(
            functools.partial(slots_kernel, capacity, slots),
            out_shape=jax.ShapeDtypeStruct(expert_idx.shape, jnp.int32),
            name="slots",
        )(expert_idx, base.reshape(1, num_experts, 1))
        w_router_t = jnp.swapaxes(w_router, 1, 2)
        hidden = x_in
        for layer in range(layers):
            h1, b = attention(layer, hidden, pad_mask, rel_bias, norm_scale, w_query, w_key, w_value, w_attn_out)
            hidden = moe(layer, 'ep', peers, capacity, pos, expert_idx, norm_scale, w_router_t, h1, b, w_in, w_out)
        return hidden

    return jax.shard_map(per_device, mesh=mesh, in_specs=(token_spec, token_spec, P(), P(None, ('dp', 'ep')), P(), P(), P(), P(), P(), P(), P(None, 'ep'), P(None, 'ep')), out_specs=token_spec, check_vma=False)
```

time: 574 us -> 528 us (0.920)
  Pallas kernels: 557 us -> 523 us
  local copies, waits for them, and re-layouts: 15.7 us -> 4.53 us
    pallas_call x2, Pallas kernels: 98.2 us -> 65.5 us  [attention(): pl.pallas_call(functools.partial(attn_kernel, layer, head_dim), grid=(pai...]
    reshape x6 -> x0, local copies, waits for them, and re-layouts: 9.56 us -> none  [the longest x1 3.33 us: per_device(): pos_col = pos.reshape(layers, num_seqs, seq_len, 1)]
where the time goes in v3:
time: 528 us
  Pallas kernels  523 us (99%)
    pallas_call x2, Pallas kernels, moe(): pl.pallas_call(functools.partial(moe_kernel, layer, axis), in_specs=[near...  456 us
    pallas_call x2, Pallas kernels, attention(): pl.pallas_call(functools.partial(attn_kernel, layer, head_dim), grid=(pai...  65.5 us

profile of v3, /device:TPU:21, one launch (start us, length us, event | category | flops | bytes accessed | tf_op | source)
XLA Modules:
  0.0 528.2 jit_solution(9723552712594953809)
XLA Ops:
  0.0 1.3 copy.17.e_ref
  1.3 0.6 fusion.8.base_ref
  1.9 1.9 slots.1.pos_ref
  3.9 32.7 %attn.2 = (bf16[3,512,768]{2,1,0:T(8,128)(2,1)}, bf16[3,512,768]{2,1,0:T(8,128)(2,1)}) custom-call(bf16[3,512,768]{2,1,0:T(8,128)(2,1)} %x_ref.1, s32[3,512]{1,0:T(4,128)} %mask_ref.3, f32[12,512,512]{2,1,0:T(8,128)} %bias_ref.3, f32[2,2,768]{2,1,0:T(2,128)} %gain_ref.7, bf16[2,768,768]{2,1,0:T(8,128)(2,1)} %wq_ref.3, bf16[2,768,768]{2,1,0:T(8,128)(2,1)} %wk_ref.3, ...), custom_call_target="tpu_custom_call" | custom-call | flops 9663676416 | bytes 33554432 | tf_op jit(solution)/shard_map/attn/pallas_call | solution.py:94
  36.6 231.8 %moe.2.x_ref = bf16[3,512,768]{2,1,0:T(8,128)(2,1)} custom-call(s32[2,3,512]{2,1,0:T(4,128)} %slots.1.pos_ref, s32[2,3,512]{2,1,0:T(4,128)} %copy.17.e_ref, f32[2,2,768]{2,1,0:T(2,128)} %gain_ref.7, f32[2,64,768]{2,1,0:T(8,128)} %bitcast.1, bf16[3,512,768]{2,1,0:T(8,128)(2,1)} %get-tuple-element.9.h1_ref, bf16[3,512,768]{2,1,0:T(8,128)(2,1)} %get-tuple-element.10.b_ref, ...), custom_call_target="tpu_custom_call" | custom-call | flops 28991029248 | bytes 50331648 | tf_op jit(solution)/shard_map/moe/pallas_call | solution.py:237
  268.4 32.8 %attn.3 = (bf16[3,512,768]{2,1,0:T(8,128)(2,1)}, bf16[3,512,768]{2,1,0:T(8,128)(2,1)}) custom-call(bf16[3,512,768]{2,1,0:T(8,128)(2,1)} %moe.2.x_ref, s32[3,512]{1,0:T(4,128)} %mask_ref.3, f32[12,512,512]{2,1,0:T(8,128)} %bias_ref.3, f32[2,2,768]{2,1,0:T(2,128)} %gain_ref.7, bf16[2,768,768]{2,1,0:T(8,128)(2,1)} %wq_ref.3, bf16[2,768,768]{2,1,0:T(8,128)(2,1)} %wk_ref.3, ...), custom_call_target="tpu_custom_call" | custom-call | flops 9663676416 | bytes 33554432 | tf_op jit(solution)/shard_map/attn/pallas_call | solution.py:94
  301.2 223.7 %moe.3 = bf16[3,512,768]{2,1,0:T(8,128)(2,1)} custom-call(s32[2,3,512]{2,1,0:T(4,128)} %slots.1.pos_ref, s32[2,3,512]{2,1,0:T(4,128)} %copy.17.e_ref, f32[2,2,768]{2,1,0:T(2,128)} %gain_ref.7, f32[2,64,768]{2,1,0:T(8,128)} %bitcast.2, bf16[3,512,768]{2,1,0:T(8,128)(2,1)} %get-tuple-element.11.h1_ref, bf16[3,512,768]{2,1,0:T(8,128)(2,1)} %get-tuple-element.12.b_ref, ...), custom_call_target="tpu_custom_call" | custom-call | flops 28991029248 | bytes 50331648 | tf_op jit(solution)/shard_map/moe/pallas_call | solution.py:237
  525.0 3.2 copy.21

commit v4 on v3

--- a/solution.py
+++ b/solution.py
@@ -19,39 +19,60 @@
     return hid32 * lax.rsqrt(jnp.mean(hid32 * hid32, axis=-1, keepdims=True) + NORM_EPS) * gain
 
 
-def slots_kernel(capacity, drop, e_ref, base_ref, pos_ref):
-    layers, num_seqs, seq_len = e_ref.shape
-    num_experts = base_ref.shape[1]
+def slots_kernel(capacity, mine, num_experts, e_ref, pos_ref):
+    num_seqs, layers, seq_len = e_ref.shape
+    drop = num_experts * capacity
     row = lax.broadcasted_iota(jnp.int32, (LANES, LANES), 0)
     col = lax.broadcasted_iota(jnp.int32, (LANES, LANES), 1)
     upper = (row <= col).astype(F32).astype(BF16)
     experts = lax.broadcasted_iota(jnp.int32, (num_experts, LANES), 0)
+    number = lax.broadcasted_iota(jnp.int32, (num_experts, 1), 0).astype(F32)
+    owner = jnp.floor((number + 0.5) * (1.0 / mine))
+    base_of = (number - owner * mine) * (num_experts // mine * capacity) + owner * capacity
     for layer in range(layers):
         carry = jnp.zeros((num_experts, 1), F32)
         for blk in range(num_seqs * seq_len // LANES):
             seq, first = divmod(blk * LANES, seq_len)
-            hit = experts == e_ref[layer, seq:seq + 1, first:first + LANES]
+            hit = experts == e_ref[seq, layer:layer + 1, first:first + LANES]
             hot = hit.astype(F32)
             cum = jnp.dot(hot.astype(BF16), upper, preferred_element_type=F32) + (carry - 1.0)
             slot = jnp.sum(hot * cum, axis=0, keepdims=True)
-            base = jnp.sum(hot * base_ref[0], axis=0, keepdims=True)
+            base = jnp.sum(hot * base_of, axis=0, keepdims=True)
             carry = carry + jnp.sum(hot, axis=1, keepdims=True)
-            pos_ref[layer, seq:seq + 1, first:first + LANES] = jnp.where(slot < capacity, base + slot, float(drop)).astype(jnp.int32)
-
-
-def attn_kernel(layer, head_dim, x_ref, mask_ref, bias_ref, gain_ref, wq_ref, wk_ref, wv_ref, wo_ref,
-                h1_ref, b_ref, q_s, k_s, v_s, ctx_s):
+            pos_ref[seq, layer:layer + 1, first:first + LANES] = jnp.where(slot < capacity, base + slot, float(drop)).astype(jnp.int32)
+
+
+def attn_kernel(layer, head_dim, x_hbm, mask_ref, bias_ref, gain_ref, wq_hbm, wk_hbm, wv_hbm, wo_hbm,
+                h1_hbm, b_hbm, x_ref, h1_ref, b_ref, w_ref, q_s, k_s, v_s, ctx_s, x_sem, w_sem, out_sem):
     pair = pl.program_id(0)
     pairs = pl.num_programs(0)
     n_pairs, num_seqs, _, width = q_s.shape
+    x_in = lambda seq: pltpu.make_async_copy(x_hbm.at[seq], x_ref.at[seq], x_sem.at[seq])
+    weight = lambda i: pltpu.make_async_copy((wq_hbm, wk_hbm, wv_hbm, wo_hbm)[i].at[layer], w_ref.at[i], w_sem.at[i])
+    h1_out = lambda seq: pltpu.make_async_copy(h1_ref.at[seq], h1_hbm.at[seq], out_sem.at[0, seq])
+    b_out = lambda seq: pltpu.make_async_copy(b_ref.at[seq], b_hbm.at[seq], out_sem.at[1, seq])
 
     @pl.when(pair == 0)
     def _():
+        x_in(0).start()
+        for i in range(3):
+            weight(i).start()
+        for seq in range(1, num_seqs):
+            x_in(seq).start()
+        weight(3).start()
+
         @pl.loop(0, num_seqs)
         def _(seq):
+            x_in(seq).wait()
             a = rms(x_ref[seq].astype(F32), gain_ref[layer, 0:1, :]).astype(BF16)
-            for w_ref, dst in ((wq_ref, q_s), (wk_ref, k_s), (wv_ref, v_s)):
-                rows = jnp.dot(a, w_ref[...], preferred_element_type=F32).astype(BF16)
+
+            @pl.when(seq == 0)
+            def _():
+                for i in range(3):
+                    weight(i).wait()
+
+            for i, dst in enumerate((q_s, k_s, v_s)):
+                rows = jnp.dot(a, w_ref[i], preferred_element_type=F32).astype(BF16)
                 for j in range(n_pairs):
                     dst[j, seq] = rows[:, j * width:(j + 1) * width]
 
@@ -73,12 +94,20 @@
 
     @pl.when(pair == pairs - 1)
     def _():
+        weight(3).wait()
+
         @pl.loop(0, num_seqs)
         def _(seq):
-            o = jnp.dot(ctx_s[seq], wo_ref[...], preferred_element_type=F32)
+            o = jnp.dot(ctx_s[seq], w_ref[3], preferred_element_type=F32)
             h1 = (x_ref[seq].astype(F32) + o).astype(BF16)
             h1_ref[seq] = h1
             b_ref[seq] = rms(h1.astype(F32), gain_ref[layer, 1:2, :]).astype(BF16)
+            h1_out(seq).start()
+            b_out(seq).start()
+
+        for seq in range(num_seqs):
+            h1_out(seq).wait()
+            b_out(seq).wait()
 
 
 def attention(layer, x, mask, rel_bias, gains, wq, wk, wv, wo):
@@ -89,27 +118,26 @@
     per = LANES // head_dim
     pairs = num_heads // per
     full = lambda *shape: pl.BlockSpec(shape, lambda p: (0,) * len(shape))
-    of_layer = lambda *shape: pl.BlockSpec((None,) + shape, lambda p: (layer,) + (0,) * len(shape))
+    hbm = pl.BlockSpec(memory_space=pl.ANY)
     flops = 2 * num_seqs * seq_len * (4 * model_dim * inner + 2 * seq_len * inner)
     return pl.pallas_call(
         functools.partial(attn_kernel, layer, head_dim),
         grid=(pairs,),
-        in_specs=[full(num_seqs, seq_len, model_dim), full(num_seqs, seq_len),
-                  pl.BlockSpec((per, seq_len, seq_len), lambda p: (p, 0, 0)), full(*gains.shape),
-                  of_layer(model_dim, inner), of_layer(model_dim, inner), of_layer(model_dim, inner),
-                  of_layer(inner, model_dim)],
-        out_specs=[full(num_seqs, seq_len, model_dim), full(num_seqs, seq_len, model_dim)],
+        in_specs=[hbm, full(num_seqs, seq_len), pl.BlockSpec((per, seq_len, seq_len), lambda p: (p, 0, 0)),
+                  full(*gains.shape), hbm, hbm, hbm, hbm],
+        out_specs=[hbm, hbm],
         out_shape=[jax.ShapeDtypeStruct(x.shape, BF16), jax.ShapeDtypeStruct(x.shape, BF16)],
-        scratch_shapes=[pltpu.VMEM((pairs, num_seqs, seq_len, LANES), BF16)] * 3
-        + [pltpu.VMEM((num_seqs, seq_len, inner), BF16)],
+        scratch_shapes=[pltpu.VMEM(x.shape, BF16)] * 3 + [pltpu.VMEM((4, model_dim, inner), BF16)]
+        + [pltpu.VMEM((pairs, num_seqs, seq_len, LANES), BF16)] * 3 + [pltpu.VMEM((num_seqs, seq_len, inner), BF16)]
+        + [pltpu.SemaphoreType.DMA((num_seqs,)), pltpu.SemaphoreType.DMA((4,)), pltpu.SemaphoreType.DMA((2, num_seqs))],
         compiler_params=pltpu.CompilerParams(dimension_semantics=("arbitrary",), vmem_limit_bytes=60 << 20),
         cost_estimate=pl.CostEstimate(flops=flops, bytes_accessed=32 << 20, transcendentals=num_seqs * num_heads * seq_len * seq_len),
         name="attn",
     )(x, mask, rel_bias, gains, wq, wk, wv, wo)
 
 
-def moe_kernel(layer, axis, pos_ref, e_ref, gain_ref, wr_ref, h1_ref, b_ref, w_in_ref, w_out_ref, out_ref,
-               packed, recv, ret, w_in_buf, w_out_buf, acc, u_acc, pos_col, gate_col, out_send, out_recv, back_send, back_recv, w_sem):
+def moe_kernel(layer, axis, pos_ref, e_ref, gain_ref, wr_ref, b_ref, h1_hbm, w_in_ref, w_out_ref, out_ref,
+               h1_ref, packed, recv, ret, w_in_buf, w_out_buf, acc, u_acc, pos_col, gate_col, out_send, out_recv, back_send, back_recv, w_sem, h1_sem):
     mine, peers, capacity, dim = packed.shape
     num_seqs, seq_len, _ = b_ref.shape
     ff = w_in_buf.shape[2]
@@ -137,6 +165,8 @@
         def _(shift):
             fn(other(shift))
 
+    h1_in = pltpu.make_async_copy(h1_hbm, h1_ref, h1_sem)
+    h1_in.start()
     for k in range(min(2, mine)):
         for copy in weights(k):
             copy.start()
@@ -154,25 +184,34 @@
             want = lax.broadcasted_iota(jnp.int32, (half * capacity, seq_len), 0) + first
             total = None
             for s in range(num_seqs):
-                hot = (want == pos_ref[layer, s:s + 1, :]).astype(F32).astype(BF16)
+                hot = (want == pos_ref[s, layer:layer + 1, :]).astype(F32).astype(BF16)
                 term = jnp.dot(hot, b_ref[s], preferred_element_type=F32)
                 total = term if total is None else total + term
             packed[k, pl.ds(part * half, half)] = total.astype(BF16).reshape(half, capacity, dim)
-        each_peer(lambda peer: there(k, peer, me).start())
+
+            @pl.loop(0, half)
+            def _(i):
+                peer = part * half + lax.rem(me + i, half)
+
+                @pl.when(peer != me)
+                def _():
+                    there(k, peer, me).start()
+
         recv[k, me] = packed[k, me]
 
     u_acc[...] = jnp.zeros_like(u_acc)
+    h1_in.wait()
     column = lambda row: jnp.broadcast_to(row, (LANES, row.shape[1])).T[:, :1]
     for s in range(num_seqs):
         @pl.loop(0, seq_len // 256)
         def _(part):
             tok = pl.ds(pl.multiple_of(part * 256, 256), 256)
-            pos_col[s, tok, :] = column(pos_ref[layer, s:s + 1, tok].astype(F32)).astype(jnp.int32)
+            pos_col[s, tok, :] = column(pos_ref[s, layer:layer + 1, tok].astype(F32)).astype(jnp.int32)
             r = rms(h1_ref[s, tok, :].astype(F32), gain_ref[layer, 1:2, :])
             logits = lax.dot_general(wr_ref[layer], r, (((1,), (1,)), ((), ())),
                                      precision=lax.Precision.HIGHEST, preferred_element_type=F32)
             ex = jnp.exp(logits - jnp.max(logits, axis=0, keepdims=True))
-            chosen = lax.broadcasted_iota(jnp.int32, ex.shape, 0) == e_ref[layer, s:s + 1, tok]
+            chosen = lax.broadcasted_iota(jnp.int32, ex.shape, 0) == e_ref[s, layer:layer + 1, tok]
             gate = jnp.sum(jnp.where(chosen, ex, 0.0), axis=0, keepdims=True) / jnp.sum(ex, axis=0, keepdims=True)
             gate_col[s, tok, :] = column(gate)
 
@@ -200,15 +239,21 @@
             for copy in weights(k + 2):
                 copy.start()
 
-    def gather_back(k, last):
-        each_peer(lambda peer: back(k, peer, peer).wait_recv())
+    def gather_back(k, first, count, last):
+        @pl.loop(first, first + count)
+        def _(peer):
+            @pl.when(peer != me)
+            def _():
+                back(k, peer, peer).wait_recv()
+
         for s in range(num_seqs):
             @pl.loop(0, seq_len // 256)
             def _(part):
                 tok = pl.ds(pl.multiple_of(part * 256, 256), 256)
-                want = lax.broadcasted_iota(jnp.int32, (256, rows), 1) + k * rows
+                want = lax.broadcasted_iota(jnp.int32, (256, count * capacity), 1) + (k * rows + first * capacity)
                 hot = (want == pos_col[s, tok, :]).astype(F32).astype(BF16)
-                u = jnp.dot(hot, ret[k].reshape(rows, dim), preferred_element_type=F32) + u_acc[s, tok, :].astype(F32)
+                u = jnp.dot(hot, ret[k, pl.ds(first, count)].reshape(count * capacity, dim), preferred_element_type=F32)
+                u = u + u_acc[s, tok, :].astype(F32)
                 if last:
                     out_ref[s, tok, :] = (h1_ref[s, tok, :].astype(F32) + gate_col[s, tok, :] * u).astype(BF16)
                 else:
@@ -216,9 +261,10 @@
 
     @pl.loop(0, mine - 1)
     def _(k):
-        gather_back(k, False)
-
-    gather_back(mine - 1, True)
+        gather_back(k, 0, peers, False)
+
+    gather_back(mine - 1, 0, half, False)
+    gather_back(mine - 1, half, peers - half, True)
 
     @pl.loop(0, mine)
     def _(k):
@@ -226,7 +272,7 @@
         each_peer(lambda peer: back(k, peer, me).wait_send())
 
 
-def moe(layer, axis, peers, capacity, pos, expert_idx, gains, w_router_t, h1, b, w_in, w_out):
+def moe(layer, axis, peers, capacity, pos, ids, gains, w_router_t, h1, b, w_in, w_out):
     num_seqs, seq_len, dim = h1.shape
     mine, _, ff = w_in.shape[1:]
     rows = peers * capacity
@@ -236,17 +282,17 @@
     sems = pltpu.SemaphoreType.DMA((mine, peers))
     return pl.pallas_call(
         functools.partial(moe_kernel, layer, axis),
-        in_specs=[near] * 6 + [hbm, hbm],
+        in_specs=[near] * 5 + [hbm] * 3,
         out_specs=near,
         out_shape=jax.ShapeDtypeStruct(h1.shape, BF16),
-        scratch_shapes=[buffer, buffer, buffer, pltpu.VMEM((2, dim, ff), BF16), pltpu.VMEM((2, ff, dim), BF16),
+        scratch_shapes=[pltpu.VMEM(h1.shape, BF16), buffer, buffer, buffer, pltpu.VMEM((2, dim, ff), BF16), pltpu.VMEM((2, ff, dim), BF16),
                         pltpu.VMEM((rows, dim), F32), pltpu.VMEM((num_seqs, seq_len, dim), BF16),
                         pltpu.VMEM((num_seqs, seq_len, 1), jnp.int32), pltpu.VMEM((num_seqs, seq_len, 1), F32),
-                        sems, sems, sems, sems, pltpu.SemaphoreType.DMA((2, 2))],
+                        sems, sems, sems, sems, pltpu.SemaphoreType.DMA((2, 2)), pltpu.SemaphoreType.DMA(())],
         compiler_params=pltpu.CompilerParams(collective_id=layer, has_side_effects=True, vmem_limit_bytes=67043328),
         cost_estimate=pl.CostEstimate(flops=4 * mine * rows * dim * ff, bytes_accessed=48 << 20, transcendentals=0),
         name="moe",
-    )(pos, expert_idx, gains, w_router_t, h1, b, w_in, w_out)
+    )(pos, ids, gains, w_router_t, b, h1, w_in, w_out)
 
 
 def solution(mesh):
@@ -260,19 +306,17 @@
         num_experts = w_router.shape[2]
         mine = num_experts // peers
         capacity = (CAP_FACTOR * tok_count + num_experts - 1) // num_experts
-        slots = num_experts * capacity
-        expert_ids = jnp.arange(num_experts, dtype=jnp.int32)
-        base = ((expert_ids % mine) * (peers * capacity) + (expert_ids // mine) * capacity).astype(F32)
+        ids = jnp.swapaxes(expert_idx, 0, 1)
         pos = pl.pallas_call(
-            functools.partial(slots_kernel, capacity, slots),
-            out_shape=jax.ShapeDtypeStruct(expert_idx.shape, jnp.int32),
+            functools.partial(slots_kernel, capacity, mine, num_experts),
+            out_shape=jax.ShapeDtypeStruct(ids.shape, jnp.int32),
             name="slots",
-        )(expert_idx, base.reshape(1, num_experts, 1))
+        )(ids)
         w_router_t = jnp.swapaxes(w_router, 1, 2)
         hidden = x_in
         for layer in range(layers):
             h1, b = attention(layer, hidden, pad_mask, rel_bias, norm_scale, w_query, w_key, w_value, w_attn_out)
-            hidden = moe(layer, 'ep', peers, capacity, pos, expert_idx, norm_scale, w_router_t, h1, b, w_in, w_out)
+            hidden = moe(layer, 'ep', peers, capacity, pos, ids, norm_scale, w_router_t, h1, b, w_in, w_out)
         return hidden
 
     return jax.shard_map(per_device, mesh=mesh, in_specs=(token_spec, token_spec, P(), P(None, ('dp', 'ep')), P(), P(), P(), P(), P(), P(), P(None, 'ep'), P(None, 'ep')), out_specs=token_spec, check_vma=False)

time: 528 us -> 522 us (0.989)
  no operation moved by 1% of the time
where the time goes in v4:
time: 522 us
  Pallas kernels  518 us (99%)
    pallas_call x2, Pallas kernels, moe(): pl.pallas_call(functools.partial(moe_kernel, layer, axis), in_specs=[near...  453 us
    pallas_call x2, Pallas kernels, attention(): pl.pallas_call(functools.partial(attn_kernel, layer, head_dim), grid=(pai...  64.2 us

profile of v4, /device:TPU:21, one launch (start us, length us, event | category | flops | bytes accessed | tf_op | source)
XLA Modules:
  0.0 521.6 jit_solution(11313524955516941988)
XLA Ops:
  0.0 1.7 slots.1.pos_ref
  1.7 32.1 %attn.2 = (bf16[3,512,768]{2,1,0:T(8,128)(2,1)}, bf16[3,512,768]{2,1,0:T(8,128)(2,1)}) custom-call(bf16[3,512,768]{2,1,0:T(8,128)(2,1)} %x_hbm.1, s32[3,512]{1,0:T(4,128)} %mask_ref.3, f32[12,512,512]{2,1,0:T(8,128)} %bias_ref.3, f32[2,2,768]{2,1,0:T(2,128)} %gain_ref.7, bf16[2,768,768]{2,1,0:T(8,128)(2,1)} %wq_hbm.3, bf16[2,768,768]{2,1,0:T(8,128)(2,1)} %wk_hbm.3, ...), custom_call_target="tpu_custom_call" | custom-call | flops 9663676416 | bytes 33554432 | tf_op jit(solution)/shard_map/attn/pallas_call | solution.py:123
  33.8 225.0 %moe.2.x_hbm = bf16[3,512,768]{2,1,0:T(8,128)(2,1)} custom-call(s32[3,2,512]{2,1,0:T(2,128)} %slots.1.pos_ref, s32[3,2,512]{2,1,0:T(2,128)} %bitcast.3, f32[2,2,768]{2,1,0:T(2,128)} %gain_ref.7, f32[2,64,768]{2,1,0:T(8,128)} %bitcast.5, bf16[3,512,768]{2,1,0:T(8,128)(2,1)} %get-tuple-element.9.b_ref, bf16[3,512,768]{2,1,0:T(8,128)(2,1)} %get-tuple-element.10.h1_hbm, ...), custom_call_target="tpu_custom_call" | custom-call | flops 28991029248 | bytes 50331648 | tf_op jit(solution)/shard_map/moe/pallas_call | solution.py:283
  258.8 32.1 %attn.3 = (bf16[3,512,768]{2,1,0:T(8,128)(2,1)}, bf16[3,512,768]{2,1,0:T(8,128)(2,1)}) custom-call(bf16[3,512,768]{2,1,0:T(8,128)(2,1)} %moe.2.x_hbm, s32[3,512]{1,0:T(4,128)} %mask_ref.3, f32[12,512,512]{2,1,0:T(8,128)} %bias_ref.3, f32[2,2,768]{2,1,0:T(2,128)} %gain_ref.7, bf16[2,768,768]{2,1,0:T(8,128)(2,1)} %wq_hbm.3, bf16[2,768,768]{2,1,0:T(8,128)(2,1)} %wk_hbm.3, ...), custom_call_target="tpu_custom_call" | custom-call | flops 9663676416 | bytes 33554432 | tf_op jit(solution)/shard_map/attn/pallas_call | solution.py:123
  290.9 227.5 %moe.3 = bf16[3,512,768]{2,1,0:T(8,128)(2,1)} custom-call(s32[3,2,512]{2,1,0:T(2,128)} %slots.1.pos_ref, s32[3,2,512]{2,1,0:T(2,128)} %bitcast.4, f32[2,2,768]{2,1,0:T(2,128)} %gain_ref.7, f32[2,64,768]{2,1,0:T(8,128)} %bitcast.6, bf16[3,512,768]{2,1,0:T(8,128)(2,1)} %get-tuple-element.11.b_ref, bf16[3,512,768]{2,1,0:T(8,128)(2,1)} %get-tuple-element.12.h1_hbm, ...), custom_call_target="tpu_custom_call" | custom-call | flops 28991029248 | bytes 50331648 | tf_op jit(solution)/shard_map/moe/pallas_call | solution.py:283
  518.4 3.2 copy.14

commit v5 on v4

--- a/solution.py
+++ b/solution.py
@@ -136,8 +136,8 @@
     )(x, mask, rel_bias, gains, wq, wk, wv, wo)
 
 
-def moe_kernel(layer, axis, pos_ref, e_ref, gain_ref, wr_ref, b_ref, h1_hbm, w_in_ref, w_out_ref, out_ref,
-               h1_ref, packed, recv, ret, w_in_buf, w_out_buf, acc, u_acc, pos_col, gate_col, out_send, out_recv, back_send, back_recv, w_sem, h1_sem):
+def moe_kernel(layer, axis, pos_ref, e_ref, gain_ref, wr_ref, b_hbm, h1_hbm, w_in_ref, w_out_ref, out_ref,
+               b_ref, h1_ref, packed, recv, ret, w_in_buf, w_out_buf, acc, u_acc, pos_col, gate_col, out_send, out_recv, back_send, back_recv, w_sem, x_sem):
     mine, peers, capacity, dim = packed.shape
     num_seqs, seq_len, _ = b_ref.shape
     ff = w_in_buf.shape[2]
@@ -165,38 +165,48 @@
         def _(shift):
             fn(other(shift))
 
-    h1_in = pltpu.make_async_copy(h1_hbm, h1_ref, h1_sem)
+    b_in = pltpu.make_async_copy(b_hbm, b_ref, x_sem.at[0])
+    h1_in = pltpu.make_async_copy(h1_hbm, h1_ref, x_sem.at[1])
+    b_in.start()
+    barrier = pltpu.get_barrier_semaphore()
+    each_peer(lambda peer: pl.semaphore_signal(barrier, inc=1, device_id={axis: peer}, device_id_type=pl.DeviceIdType.MESH))
+    half = peers // 2
+
+    def pack(k, part):
+        first = k * rows + part * (half * capacity)
+        want = lax.broadcasted_iota(jnp.int32, (half * capacity, seq_len), 0) + first
+        total = None
+        for s in range(num_seqs):
+            hot = (want == pos_ref[s, layer:layer + 1, :]).astype(F32).astype(BF16)
+            term = jnp.dot(hot, b_ref[s], preferred_element_type=F32)
+            total = term if total is None else total + term
+        packed[k, pl.ds(part * half, half)] = total.astype(BF16).reshape(half, capacity, dim)
+
+    def send(k, part):
+        @pl.loop(0, half)
+        def _(i):
+            peer = part * half + lax.rem(me + i, half)
+
+            @pl.when(peer != me)
+            def _():
+                there(k, peer, me).start()
+
+    b_in.wait()
+    pack(0, 0)
+    pl.semaphore_wait(barrier, peers - 1)
+    send(0, 0)
     h1_in.start()
     for k in range(min(2, mine)):
         for copy in weights(k):
             copy.start()
 
-    barrier = pltpu.get_barrier_semaphore()
-    each_peer(lambda peer: pl.semaphore_signal(barrier, inc=1, device_id={axis: peer}, device_id_type=pl.DeviceIdType.MESH))
-    pl.semaphore_wait(barrier, peers - 1)
-
-    half = peers // 2
+    @pl.loop(1, 2 * mine)
+    def _(step):
+        pack(step // 2, step % 2)
+        send(step // 2, step % 2)
+
     @pl.loop(0, mine)
     def _(k):
-        @pl.loop(0, 2)
-        def _(part):
-            first = k * rows + part * (half * capacity)
-            want = lax.broadcasted_iota(jnp.int32, (half * capacity, seq_len), 0) + first
-            total = None
-            for s in range(num_seqs):
-                hot = (want == pos_ref[s, layer:layer + 1, :]).astype(F32).astype(BF16)
-                term = jnp.dot(hot, b_ref[s], preferred_element_type=F32)
-                total = term if total is None else total + term
-            packed[k, pl.ds(part * half, half)] = total.astype(BF16).reshape(half, capacity, dim)
-
-            @pl.loop(0, half)
-            def _(i):
-                peer = part * half + lax.rem(me + i, half)
-
-                @pl.when(peer != me)
-                def _():
-                    there(k, peer, me).start()
-
         recv[k, me] = packed[k, me]
 
     u_acc[...] = jnp.zeros_like(u_acc)
@@ -282,17 +292,37 @@
     sems = pltpu.SemaphoreType.DMA((mine, peers))
     return pl.pallas_call(
         functools.partial(moe_kernel, layer, axis),
-        in_specs=[near] * 5 + [hbm] * 3,
+        in_specs=[near] * 4 + [hbm] * 4,
         out_specs=near,
         out_shape=jax.ShapeDtypeStruct(h1.shape, BF16),
-        scratch_shapes=[pltpu.VMEM(h1.shape, BF16), buffer, buffer, buffer, pltpu.VMEM((2, dim, ff), BF16), pltpu.VMEM((2, ff, dim), BF16),
+        scratch_shapes=[pltpu.VMEM(h1.shape, BF16), pltpu.VMEM(h1.shape, BF16), buffer, buffer, buffer, pltpu.VMEM((2, dim, ff), BF16), pltpu.VMEM((2, ff, dim), BF16),
                         pltpu.VMEM((rows, dim), F32), pltpu.VMEM((num_seqs, seq_len, dim), BF16),
                         pltpu.VMEM((num_seqs, seq_len, 1), jnp.int32), pltpu.VMEM((num_seqs, seq_len, 1), F32),
-                        sems, sems, sems, sems, pltpu.SemaphoreType.DMA((2, 2)), pltpu.SemaphoreType.DMA(())],
+                        sems, sems, sems, sems, pltpu.SemaphoreType.DMA((2, 2)), pltpu.SemaphoreType.DMA((2,))],
         compiler_params=pltpu.CompilerParams(collective_id=layer, has_side_effects=True, vmem_limit_bytes=67043328),
         cost_estimate=pl.CostEstimate(flops=4 * mine * rows * dim * ff, bytes_accessed=48 << 20, transcendentals=0),
         name="moe",
     )(pos, ids, gains, w_router_t, b, h1, w_in, w_out)
+
+
+def out_kernel(x_hbm, out_hbm, buf, sems):
+    load = lambda i: pltpu.make_async_copy(x_hbm.at[i], buf.at[i], sems.at[0, i])
+    store = lambda i: pltpu.make_async_copy(buf.at[i], out_hbm.at[i], sems.at[1, i])
+    for i in range(buf.shape[0]):
+        load(i).start()
+    for i in range(buf.shape[0]):
+        load(i).wait()
+        store(i).start()
+    for i in range(buf.shape[0]):
+        store(i).wait()
+
+
+def hand_out(x):
+    hbm = pl.BlockSpec(memory_space=pl.ANY)
+    return pl.pallas_call(
+        out_kernel, in_specs=[hbm], out_specs=hbm, out_shape=jax.ShapeDtypeStruct(x.shape, x.dtype),
+        scratch_shapes=[pltpu.VMEM(x.shape, x.dtype), pltpu.SemaphoreType.DMA((2, x.shape[0]))], name="out",
+    )(x)
 
 
 def solution(mesh):
@@ -317,6 +347,6 @@
         for layer in range(layers):
             h1, b = attention(layer, hidden, pad_mask, rel_bias, norm_scale, w_query, w_key, w_value, w_attn_out)
             hidden = moe(layer, 'ep', peers, capacity, pos, ids, norm_scale, w_router_t, h1, b, w_in, w_out)
-        return hidden
+        return hand_out(hidden)
 
     return jax.shard_map(per_device, mesh=mesh, in_specs=(token_spec, token_spec, P(), P(None, ('dp', 'ep')), P(), P(), P(), P(), P(), P(), P(None, 'ep'), P(None, 'ep')), out_specs=token_spec, check_vma=False)

time: 522 us -> 519 us (level)
  no operation moved by 1% of the time
where the time goes in v5:
time: 519 us; the launch traced here: 516 us
  Pallas kernels  516 us (99%)
    pallas_call x2, Pallas kernels, moe(): pl.pallas_call(functools.partial(moe_kernel, layer, axis), in_specs=[near...  448 us
    pallas_call x2, Pallas kernels, attention(): pl.pallas_call(functools.partial(attn_kernel, layer, head_dim), grid=(pai...  64.1 us

profile of v5, /device:TPU:21, one launch (start us, length us, event | category | flops | bytes accessed | tf_op | source)
XLA Modules:
  0.0 516.3 jit_solution(1036218857008884081)
XLA Ops:
  0.0 1.7 slots.1.pos_ref
  1.7 32.1 %attn.2 = (bf16[3,512,768]{2,1,0:T(8,128)(2,1)}, bf16[3,512,768]{2,1,0:T(8,128)(2,1)}) custom-call(bf16[3,512,768]{2,1,0:T(8,128)(2,1)} %x_hbm.1, s32[3,512]{1,0:T(4,128)} %mask_ref.3, f32[12,512,512]{2,1,0:T(8,128)} %bias_ref.3, f32[2,2,768]{2,1,0:T(2,128)} %gain_ref.7, bf16[2,768,768]{2,1,0:T(8,128)(2,1)} %wq_hbm.3, bf16[2,768,768]{2,1,0:T(8,128)(2,1)} %wk_hbm.3, ...), custom_call_target="tpu_custom_call" | custom-call | flops 9663676416 | bytes 33554432 | tf_op jit(solution)/shard_map/attn/pallas_call | solution.py:123
  33.8 225.5 %moe.2.x_hbm = bf16[3,512,768]{2,1,0:T(8,128)(2,1)} custom-call(s32[3,2,512]{2,1,0:T(2,128)} %slots.1.pos_ref, s32[3,2,512]{2,1,0:T(2,128)} %bitcast.3, f32[2,2,768]{2,1,0:T(2,128)} %gain_ref.7, f32[2,64,768]{2,1,0:T(8,128)} %bitcast.5, bf16[3,512,768]{2,1,0:T(8,128)(2,1)} %get-tuple-element.9.b_hbm, bf16[3,512,768]{2,1,0:T(8,128)(2,1)} %get-tuple-element.10.h1_hbm, ...), custom_call_target="tpu_custom_call" | custom-call | flops 28991029248 | bytes 50331648 | tf_op jit(solution)/shard_map/moe/pallas_call | solution.py:293
  259.3 32.1 %attn.3 = (bf16[3,512,768]{2,1,0:T(8,128)(2,1)}, bf16[3,512,768]{2,1,0:T(8,128)(2,1)}) custom-call(bf16[3,512,768]{2,1,0:T(8,128)(2,1)} %moe.2.x_hbm, s32[3,512]{1,0:T(4,128)} %mask_ref.3, f32[12,512,512]{2,1,0:T(8,128)} %bias_ref.3, f32[2,2,768]{2,1,0:T(2,128)} %gain_ref.7, bf16[2,768,768]{2,1,0:T(8,128)(2,1)} %wq_hbm.3, bf16[2,768,768]{2,1,0:T(8,128)(2,1)} %wk_hbm.3, ...), custom_call_target="tpu_custom_call" | custom-call | flops 9663676416 | bytes 33554432 | tf_op jit(solution)/shard_map/attn/pallas_call | solution.py:123
  291.4 222.1 %moe.3.x_hbm = bf16[3,512,768]{2,1,0:T(8,128)(2,1)} custom-call(s32[3,2,512]{2,1,0:T(2,128)} %slots.1.pos_ref, s32[3,2,512]{2,1,0:T(2,128)} %bitcast.4, f32[2,2,768]{2,1,0:T(2,128)} %gain_ref.7, f32[2,64,768]{2,1,0:T(8,128)} %bitcast.6, bf16[3,512,768]{2,1,0:T(8,128)(2,1)} %get-tuple-element.11.b_hbm, bf16[3,512,768]{2,1,0:T(8,128)(2,1)} %get-tuple-element.12.h1_hbm, ...), custom_call_target="tpu_custom_call" | custom-call | flops 28991029248 | bytes 50331648 | tf_op jit(solution)/shard_map/moe/pallas_call | solution.py:293
  513.6 2.6 out.1
